TPU v7x, 256 devices: a whole 4x4x8 slice. The times are simulated.
256 devices in a mesh: group: 4 (over y), dom: 64 (over x, z, core).
Axes of the slice: x: 4, y: 4, z: 8, core: 2. Of those that a mesh axis runs over, the one named last changes fastest.
Arguments:
- features: bfloat16 [2, 65536, 1024], P(None, ('group', 'dom')), may hold values from -6 to 6
- adjacency: bfloat16 [65536, 256], P(('group', 'dom')), may hold values from -0.375 to 0.375
- tile_mask: int32 [512, 2], P(('group', 'dom')), may hold values 0 or 1
- boundary_adj: bfloat16 [65536, 1024], P(('group', 'dom')), may hold values from -0.1875 to 0.1875
- boundary_blocks: int32 [4, 64, 4, 2], P('group'), may hold values from -1 to 1
- hub_adj: bfloat16 [256, 65536], P(None, ('group', 'dom')), may hold values from -0.09375 to 0.09375
- hub_offsets: int32 [4, 256], P('group', 'dom'), may hold values from 0 to 63
- weight: bfloat16 [1024, 1024], replicated, may hold values from -0.1875 to 0.1875
- cotangent: bfloat16 [2, 65536, 1024], P(None, ('group', 'dom')), may hold values from -24 to 24
Outputs:
- activations: bfloat16 [2, 65536, 1024], P(None, ('group', 'dom'))
- input_grad: bfloat16 [2, 65536, 1024], P(None, ('group', 'dom'))
- carried_grad: bfloat16 [65536, 1024], P(('group', 'dom'))
- weight_grad: float32 [1024, 1024], P(('group', 'dom'))
Inputs may be any that keep to these rules, and one draw needn't show every extreme that they name: `tile_mask`: 1 where a tile of local edges is present.
All inputs are finite; a program needn't handle non-finite values. No bound on the sum of `tile_mask` on one device may be relied on, other than what follows from the above.
Results may differ from a plain program's by a relative error of at most 0.0067.
Values may be sent and summed in bfloat16 or wider, within the bound.
No kernel may reach another device: no remote copies, remote signals or barrier semaphores. Data moves between devices by JAX's collectives and lax.ppermute only.
A program may use at most 64 MiB of HBM per device.

v0:
```python
import jax
import jax.numpy as jnp
from jax import lax
from jax.experimental import pallas as pl
from jax.experimental.pallas import tpu as pltpu
from jax.sharding import PartitionSpec as P


BLK = 128
HUB_DEV = 4
CORES = 2
XS = 4
ZS = 8
GROUPS = 4
F32 = jnp.float32
BF16 = jnp.bfloat16


def dom_index(x, z, c):
    return (x * ZS + z) * CORES + c


def dom_pairs(target):
    pairs = []
    for x in range(XS):
        for z in range(ZS):
            for c in range(CORES):
                pairs.append((dom_index(x, z, c), target(x, z, c)))
    return pairs


def swap(v):
    return lax.ppermute(v, "dom", dom_pairs(lambda x, z, c: dom_index(x, z, 1 - c)))


def along_x(v, k):
    return lax.ppermute(v, "dom", dom_pairs(lambda x, z, c: dom_index((x + k) % XS, z, c)))


def across_z(v, bit):
    return lax.ppermute(v, "dom", dom_pairs(lambda x, z, c: dom_index(x, z ^ bit, c)))


def along_y(v, k):
    return lax.ppermute(v, "group", [(y, (y + k) % GROUPS) for y in range(GROUPS)])


def chip_step(v, even_by):
    count = XS * ZS * CORES
    pairs = []
    for d in range(count):
        to = d + (even_by if d % 2 == 0 else -even_by)
        if 0 <= to < count:
            pairs.append((d, to))
    return lax.ppermute(v, "dom", pairs)


def first_step(v):
    return chip_step(v, -2)


def second_step(v):
    return chip_step(v, 2)


def dot(a, b):
    return lax.dot_general(a, b, (((1,), (0,)), ((), ())), preferred_element_type=F32)


def dot_tn(a, b):
    return lax.dot_general(a, b, (((0,), (0,)), ((), ())), preferred_element_type=F32)


def dot_nt(a, b):
    return lax.dot_general(a, b, (((1,), (1,)), ((), ())), preferred_element_type=F32)


def relative_rows(shape, with_group, here, y):
    c = here & 1
    z = (here >> 1) & (ZS - 1)
    x = here >> 4
    r = lax.broadcasted_iota(jnp.int32, shape, 0)
    low = r & 3
    zz = z ^ (((r >> 4) & 1) + (((r >> 3) & 1) << 1) + (((r >> 2) & 1) << 2))
    xx = (x + (r >> 5)) & 3
    if with_group:
        yy = (y + (r >> 7)) & 3
        return (yy << 8) + (xx << 6) + (zz << 3) + ((c ^ (r >> 9)) << 2) + low
    return (xx << 6) + (zz << 3) + ((c ^ (r >> 7)) << 2) + low


VM = pl.BlockSpec(memory_space=pltpu.VMEM)
SM = pl.BlockSpec(memory_space=pltpu.SMEM)
ANY = pl.BlockSpec(memory_space=pl.ANY)


def call(body, specs, outs, flops, *args):
    shapes = [jax.ShapeDtypeStruct(s, d) for s, d in outs]
    moved = sum(a.size * a.dtype.itemsize for a in args) + sum(s.size * s.dtype.itemsize for s in shapes)
    kernel = pl.pallas_call(
        body,
        out_shape=shapes,
        in_specs=specs,
        out_specs=[VM] * len(shapes),
        cost_estimate=pl.CostEstimate(flops=flops, bytes_accessed=moved, transcendentals=0),
        compiler_params=pltpu.CompilerParams(vmem_limit_bytes=16 * 1024 * 1024),
    )
    return kernel(*args)


def hub_kernel(hub_ref, f_ref, rel_ref, pay_ref, f0_ref, mine_ref):
    target = relative_rows((256, 256), False, lax.axis_index("dom"), 0)
    col = lax.broadcasted_iota(jnp.int32, (256, 256), 1)
    perm = jnp.where(target == col, 1.0, 0.0).astype(BF16)
    ordered = dot(perm, hub_ref[...])
    rel = ordered.astype(BF16)
    rel_ref[...] = jnp.transpose(ordered).astype(BF16)
    for t in range(2):
        for n in range(0, 1024, 256):
            p = dot(rel, f_ref[t, :, n : n + 256])
            mine_ref[:, t * 1024 + n : t * 1024 + n + 256] = p[:128]
            pay_ref[t * 128 : t * 128 + 128, n : n + 256] = p[128:].astype(BF16)
    pay_ref[256:512, :] = f_ref[0]
    f0_ref[...] = f_ref[0]


def table_kernel(asked, present, b_ref, a_ref, roles_ref, roles_t_ref, local_ref, local_t_ref):
    c = lax.axis_index("dom") & 1
    for r in range(4):
        for b in range(2):
            total = None
            for o in (r, r ^ 1):
                for j in range(2):
                    s = 2 * o + j
                    gate = jnp.where(((r ^ c) == o) & (asked[s] == b), 1.0, 0.0)
                    term = b_ref[:, s * BLK : s * BLK + BLK].astype(F32) * gate
                    total = term if total is None else total + term
            at = (2 * r + b) * BLK
            roles_ref[:, at : at + BLK] = total.astype(BF16)
            roles_t_ref[at : at + BLK, :] = jnp.transpose(total).astype(BF16)
    for i in range(2):
        for j in range(2):
            gate = present[i, j].astype(F32)
            tile = a_ref[i * BLK : i * BLK + BLK, j * BLK : j * BLK + BLK].astype(F32) * gate
            local_ref[i * BLK : i * BLK + BLK, j * BLK : j * BLK + BLK] = tile.astype(BF16)
            local_t_ref[j * BLK : j * BLK + BLK, i * BLK : i * BLK + BLK] = jnp.transpose(tile).astype(BF16)


def open_kernel(got_ref, mine_ref, keep_ref, one_ref, two_ref, three_ref):
    for t in range(2):
        lanes = slice(t * 1024, t * 1024 + 1024)
        part = mine_ref[:, lanes] + got_ref[t * 128 : t * 128 + 128, :].astype(F32)
        keep_ref[:, lanes] = part[:32]
        one_ref[:, lanes] = part[32:64].astype(BF16)
        two_ref[:, lanes] = part[64:96].astype(BF16)
        three_ref[:, lanes] = part[96:].astype(BF16)


def total_kernel(after, roles, local, f_ref, pair_ref, far_ref, first_ref, second_ref, out_ref):
    for n in range(0, 1024, 256):
        lanes = slice(n, n + 256)
        bound = (
            dot(roles[:, :256], pair_ref[256:512, lanes])
            + dot(roles[:, 256:512], far_ref[:, lanes])
            + dot(roles[:, 512:768], first_ref[:, lanes])
            + dot(roles[:, 768:], second_ref[:, lanes])
        )
        for t in range(2):
            out_ref[t * 256 : t * 256 + 256, lanes] = bound + dot(local[...], f_ref[t, :, lanes])


def agg_kernel(offs, total_ref, own_ref, g1_ref, g2_ref, g3_ref, agg_ref):
    hubs = own_ref[...] + (g1_ref[...].astype(F32) + g2_ref[...].astype(F32) + g3_ref[...].astype(F32))
    ids = lax.broadcasted_iota(jnp.int32, (64, 1024), 0)
    for t in range(2):
        for i in range(HUB_DEV):
            at = t * 256 + i * 64
            extra = jnp.where(ids == offs[0, i], hubs[i : i + 1, t * 1024 : t * 1024 + 1024], 0.0)
            agg_ref[at : at + 64, :] = (total_ref[at : at + 64, :] + extra).astype(BF16)


def send_kernel(offs, roles_t, dagg_ref, mirror_ref, first_ref):
    cols = lax.broadcasted_iota(jnp.int32, (8, 256), 1)
    rows = lax.broadcasted_iota(jnp.int32, (8, 256), 0)
    where = jnp.where(
        rows == 0, offs[0, 0], jnp.where(rows == 1, offs[0, 1], jnp.where(rows == 2, offs[0, 2], offs[0, 3]))
    )
    pick = jnp.where((cols == rows * 64 + where) & (rows < HUB_DEV), 1.0, 0.0).astype(BF16)
    for t in range(2):
        d = dagg_ref[t * 256 : t * 256 + 256, :]
        mirror_ref[:, t * 1024 : t * 1024 + 1024] = dot(pick, d)[:HUB_DEV].astype(BF16)
        first_ref[t * 256 : t * 256 + 256, :] = dot(roles_t[768:, :], d).astype(BF16)


def pair_kernel(roles_t, dagg_ref, out_ref):
    for r in range(2):
        for t in range(2):
            at = (2 * r + t) * 256
            out_ref[at : at + 256, :] = dot(
                roles_t[r * 256 : r * 256 + 256, :], dagg_ref[t * 256 : t * 256 + 256, :]
            ).astype(BF16)


def through_kernel(roles_t, dagg_ref, got_ref, out_ref):
    for t in range(2):
        rows = slice(t * 256, t * 256 + 256)
        mine = dot(roles_t[512:768, :], dagg_ref[rows, :])
        out_ref[rows, :] = (mine + got_ref[512 + t * 256 : 768 + t * 256, :].astype(F32)).astype(BF16)


def base_kernel(local_t, dagg_ref, pair_ref, first_ref, second_ref, base_ref, carried_ref):
    base_ref[:256, :] = dot(local_t[...], dagg_ref[:256, :])
    returned = pair_ref[:512, :].astype(F32) + first_ref[...].astype(F32) + second_ref[...].astype(F32)
    base_ref[256:, :] = dot(local_t[...], dagg_ref[256:, :]) + returned[:256]
    carried_ref[...] = returned[256:].astype(BF16)


def grad_kernel(base_ref, rel_t, own_ref, got_ref, out_ref):
    for t in range(2):
        lanes = slice(t * 1024, t * 1024 + 1024)
        hub = dot(rel_t[:, :128], own_ref[:, lanes]) + dot(rel_t[:, 128:], got_ref[:, lanes])
        out_ref[t] = (base_ref[t * 256 : t * 256 + 256, :] + hub).astype(BF16)


def join_kernel(own_ref, one_ref, two_ref, three_ref, out_ref):
    out_ref[:32, :] = own_ref[...]
    out_ref[32:64, :] = one_ref[...]
    out_ref[64:96, :] = two_ref[...]
    out_ref[96:, :] = three_ref[...]


def per_device(
    features,
    adjacency,
    tile_mask,
    boundary_adj,
    boundary_blocks,
    hub_adj,
    hub_offsets,
    weight,
    cotangent,
):
    steps, nodes, width = features.shape
    here = lax.axis_index("dom")
    y = lax.axis_index("group")
    both = steps * nodes
    mm = 2 * nodes * nodes * width

    rel_t, payload, first, mine = call(
        hub_kernel,
        [VM, VM],
        [((256, 256), BF16), ((512, width), BF16), ((nodes, width), BF16), ((128, 2 * width), F32)],
        2 * mm,
        hub_adj,
        features,
    )
    from_pair = swap(payload)
    from_first = first_step(first)
    from_second = second_step(first)

    asked = lax.dynamic_index_in_dim(boundary_blocks[0], here, 0, keepdims=False).reshape(8)
    roles, roles_t, local, local_t = call(
        table_kernel,
        [SM, SM, VM, VM],
        [((nodes, width), BF16), ((width, nodes), BF16), ((nodes, nodes), BF16), ((nodes, nodes), BF16)],
        mm,
        asked,
        tile_mask,
        boundary_adj,
        adjacency,
    )

    part, *sends = call(
        open_kernel,
        [VM, VM],
        [((32, 2 * width), F32)] + [((32, 2 * width), BF16)] * 3,
        mm,
        from_pair,
        mine,
    )
    gots = [along_x(sends[k - 1], k) for k in (1, 3, 2)]
    from_far = swap(from_first)
    part = part + (gots[0].astype(F32) + gots[1].astype(F32) + gots[2].astype(F32))
    marks = []
    for bit, rows in ((1, 16), (2, 8), (4, 4)):
        sent = part[rows:].astype(BF16)
        marks.append(sent)
        got = across_z(sent, bit)
        part = part[:rows] + got.astype(F32)
    sent = part.astype(BF16)
    gots = [along_y(sent, k) for k in (1, 3, 2)]

    (total,) = call(
        total_kernel,
        [ANY, VM, VM, VM, VM, VM, VM, VM],
        [((both, width), F32)],
        6 * mm,
        marks[1],
        roles,
        local,
        features,
        from_pair,
        from_far,
        from_first,
        from_second,
    )
    (agg,) = call(
        agg_kernel,
        [SM, VM, VM, VM, VM, VM],
        [((both, width), BF16)],
        mm,
        hub_offsets,
        total,
        part,
        *gots,
    )
    pre = dot_nt(agg, weight)
    sig = jax.nn.sigmoid(pre)
    act = (pre * sig).astype(BF16)
    gpre = (cotangent.reshape(both, width).astype(F32) * sig * (1.0 + pre * (1.0 - sig))).astype(BF16)

    perm = relative_rows((width, width), True, here, y) == lax.broadcasted_iota(jnp.int32, (width, width), 1)
    perm = perm.astype(BF16)
    perm = lax.optimization_barrier(perm)
    gpre_rel = lax.optimization_barrier(dot_nt(gpre, perm).astype(BF16))
    got_w = swap(dot_tn(gpre_rel[:, 512:], agg).astype(BF16))
    dagg = dot(gpre, weight).astype(BF16)

    mirror, to_first = call(
        send_kernel,
        [SM, VM, VM],
        [((HUB_DEV, 2 * width), BF16), ((both, width), BF16)],
        2 * mm,
        hub_offsets,
        roles_t,
        dagg,
    )
    gots = [along_y(mirror, k) for k in (1, 3, 2)]
    back_first = first_step(to_first)
    (to_pair,) = call(pair_kernel, [VM, VM], [((2 * both, width), BF16)], 4 * mm, roles_t, dagg)
    back_pair = swap(to_pair)
    gathered = (
        mirror.astype(F32) + (gots[0].astype(F32) + gots[1].astype(F32) + gots[2].astype(F32))
    ).astype(BF16)

    wg = lax.optimization_barrier(dot_tn(gpre_rel[:, :512], agg)) + got_w.astype(F32)
    up = along_y(wg[256:320].astype(BF16), 1)
    down = along_y(wg[320:384].astype(BF16), 3)
    to_up = jnp.concatenate([wg[128:192] + up.astype(F32), wg[192:256]], axis=0).astype(BF16)
    to_down = jnp.concatenate([wg[384:448], wg[448:512] + down.astype(F32)], axis=0).astype(BF16)
    wg = wg[:128] + along_y(to_up, 1).astype(F32) + along_y(to_down, 3).astype(F32)

    for bit in (4, 2, 1):
        gathered = jnp.concatenate([gathered, across_z(gathered, bit)], axis=0)
        gathered = lax.optimization_barrier(gathered)

    (to_second,) = call(
        through_kernel, [VM, VM, VM], [((both, width), BF16)], 2 * mm, roles_t, dagg, back_pair
    )
    back_second = second_step(to_second)

    sent = wg[32:].astype(BF16)
    gots = [along_x(sent[32 * (k - 1) : 32 * k], k) for k in (1, 3, 2)]
    wg = wg[:32] + (gots[0].astype(F32) + gots[1].astype(F32) + gots[2].astype(F32))

    gots = [along_x(gathered, -k) for k in (1, 3, 2)]
    (joined,) = call(
        join_kernel, [VM] * 4, [((128, 2 * width), BF16)], mm, gathered, gots[0], gots[2], gots[1]
    )
    other = swap(joined)
    for bit, rows in ((1, 16), (2, 8), (4, 4)):
        got = across_z(wg[rows:].astype(BF16), bit)
        wg = wg[:rows] + got.astype(F32)

    base, carried = call(
        base_kernel,
        [VM] * 5,
        [((both, width), F32), ((nodes, width), BF16)],
        2 * mm,
        local_t,
        dagg,
        back_pair,
        back_first,
        back_second,
    )
    (grads,) = call(
        grad_kernel, [VM] * 4, [((steps, nodes, width), BF16)], 2 * mm, base, rel_t, joined, other
    )
    scale = (both * GROUPS * XS * ZS * CORES) ** (-0.5)
    return act.reshape(steps, nodes, width), grads, carried, wg * scale


def solution(mesh):
    return jax.shard_map(
        per_device,
        mesh=mesh,
        in_specs=(
            P(None, ("group", "dom"), None),
            P(("group", "dom"), None),
            P(("group", "dom"), None),
            P(("group", "dom"), None),
            P("group", None, None, None),
            P(None, ("group", "dom")),
            P("group", "dom"),
            P(),
            P(None, ("group", "dom"), None),
        ),
        out_specs=(
            P(None, ("group", "dom"), None),
            P(None, ("group", "dom"), None),
            P(("group", "dom"), None),
            P(("group", "dom"), None),
        ),
        check_vma=False,
    )
```

profile of v0, /device:TPU:1, one launch (start us, length us, event | category | flops | bytes accessed | tf_op | source)
XLA Modules:
  0.0 142.2 jit_solution(11333391254718165179)
XLA Ops:
  0.7 1.4 copy-done.1
  2.0 0.9 copy-done.6
  2.9 1.4 shard_map.120
  4.3 3.2 %collective-permute-start = (bf16[512,1024]{1,0:T(8,128)(2,1)S(1)}, bf16[512,1024]{1,0:T(8,128)(2,1)S(1)}, u32[]{:S(2)}, u32[]{:S(2)}) collective-permute-start(bf16[512,1024]{1,0:T(8,128)(2,1)S(1)} %get-tuple-element.20), channel_id=1, source_target_pairs={{0,1},{1,0},{2,3},{3,2},{4,5},{5,4},{6,7},{7,6},{8,9},{9,8},{10,11... | collective-permute-start | bytes 3145736 | tf_op jit(solution)/shard_map/ppermute | solution.py:33
  7.5 2.3 %collective-permute-done.got_ref.pair_ref = bf16[512,1024]{1,0:T(8,128)(2,1)S(1)} collective-permute-done((bf16[512,1024]{1,0:T(8,128)(2,1)S(1)}, bf16[512,1024]{1,0:T(8,128)(2,1)S(1)}, u32[]{:S(2)}, u32[]{:S(2)}) %collective-permute-start) | collective-permute-done | bytes 1048608 | tf_op jit(solution)/shard_map/ppermute | solution.py:33
  10.0 2.7 %collective-permute-start.2 = (bf16[32,2048]{1,0:T(8,128)(2,1)S(1)}, bf16[32,2048]{1,0:T(8,128)(2,1)S(1)}, u32[]{:S(2)}, u32[]{:S(2)}) collective-permute-start(bf16[32,2048]{1,0:T(8,128)(2,1)S(1)} %get-tuple-element.24), channel_id=1, source_target_pairs={{0,48},{1,49},{2,50},{3,51},{4,52},{5,53},{6,54},{7,55},{8,56},{9,... | collective-permute-start | bytes 393224 | tf_op jit(solution)/shard_map/ppermute | solution.py:37
  12.7 3.2 %collective-permute-done.1 = bf16[32,2048]{1,0:T(8,128)(2,1)S(1)} collective-permute-done((bf16[32,2048]{1,0:T(8,128)(2,1)S(1)}, bf16[32,2048]{1,0:T(8,128)(2,1)S(1)}, u32[]{:S(2)}, u32[]{:S(2)}) %collective-permute-start.1) | collective-permute-done | bytes 131104 | tf_op jit(solution)/shard_map/ppermute | solution.py:37
  15.9 1.9 %collective-permute-done.2 = bf16[32,2048]{1,0:T(8,128)(2,1)S(1)} collective-permute-done((bf16[32,2048]{1,0:T(8,128)(2,1)S(1)}, bf16[32,2048]{1,0:T(8,128)(2,1)S(1)}, u32[]{:S(2)}, u32[]{:S(2)}) %collective-permute-start.2) | collective-permute-done | bytes 131104 | tf_op jit(solution)/shard_map/ppermute | solution.py:37
  17.8 0.5 collective-permute-done.3
  18.3 0.8 add_add_fusion
  19.1 1.5 %slice.168 = bf16[16,2048]{1,0:T(8,128)(2,1)} slice(f32[32,2048]{1,0:T(8,128)} %add_add_fusion), slice={[16:32], [0:2048]} | slice | bytes 131072 | tf_op jit(solution)/shard_map/slice | solution.py:286
  20.6 1.3 collective-permute-start.4
  21.9 1.3 collective-permute-start.7
  23.2 4.8 %collective-permute-start.5 = (bf16[256,1024]{1,0:T(8,128)(2,1)}, bf16[256,1024]{1,0:T(8,128)(2,1)}, u32[]{:S(2)}, u32[]{:S(2)}) collective-permute-start(bf16[256,1024]{1,0:T(8,128)(2,1)} %get-tuple-element.28), channel_id=1, source_target_pairs={{1,3},{2,0},{3,5},{4,2},{5,7},{6,4},{7,9},{8,6},{9,11},{10,8},{11,... | collective-permute-start | bytes 1572872 | tf_op jit(solution)/shard_map/ppermute | solution.py:55
  28.0 0.9 slice_add_fusion.4
  28.9 2.3 %collective-permute-start.8 = (bf16[8,2048]{1,0:T(8,128)(2,1)S(1)}, bf16[8,2048]{1,0:T(8,128)(2,1)S(1)}, u32[]{:S(2)}, u32[]{:S(2)}) collective-permute-start(bf16[8,2048]{1,0:T(8,128)(2,1)S(1)} %slice.170.after), channel_id=1, source_target_pairs={{0,4},{1,5},{2,6},{3,7},{4,0},{5,1},{6,2},{7,3},{8,12},{9,13},{10,... | collective-permute-start | bytes 98312 | tf_op jit(solution)/shard_map/ppermute | solution.py:41
  31.3 7.6 %collective-permute-done.5.first_ref = bf16[256,1024]{1,0:T(8,128)(2,1)} collective-permute-done((bf16[256,1024]{1,0:T(8,128)(2,1)}, bf16[256,1024]{1,0:T(8,128)(2,1)}, u32[]{:S(2)}, u32[]{:S(2)}) %collective-permute-start.5) | collective-permute-done | bytes 524320 | tf_op jit(solution)/shard_map/ppermute | solution.py:55
  39.2 8.1 %collective-permute-start.9 = (bf16[4,2048]{1,0:T(4,128)(2,1)S(1)}, bf16[4,2048]{1,0:T(4,128)(2,1)S(1)}, u32[]{:S(2)}, u32[]{:S(2)}) collective-permute-start(bf16[4,2048]{1,0:T(4,128)(2,1)S(1)} %slice.172), channel_id=1, source_target_pairs={{0,8},{1,9},{2,10},{3,11},{4,12},{5,13},{6,14},{7,15},{8,0},{9,1},... | collective-permute-start | bytes 49160 | tf_op jit(solution)/shard_map/ppermute | solution.py:41
  47.3 1.8 %fusion = bf16[1024,1024]{1,0:T(8,128)(2,1)} fusion(s32[1024]{0:T(1024)S(1)} %fusion.17), kind=kLoop, calls=%fused_computation.1 | loop fusion | flops 2097152 | bytes 2101248 | tf_op jit(solution)/shard_map/convert_element_type | solution.py:323
  49.4 1.0 copy-done.5
  50.4 1.1 shard_map.122
  51.5 3.0 %collective-permute-start.12 = (bf16[4,2048]{1,0:T(4,128)(2,1)S(1)}, bf16[4,2048]{1,0:T(4,128)(2,1)S(1)}, u32[]{:S(2)}, u32[]{:S(2)}) collective-permute-start(bf16[4,2048]{1,0:T(4,128)(2,1)S(1)} %get-tuple-element.40), channel_id=1, source_target_pairs={{0,128},{64,192},{128,0},{192,64},{1,129},{65,193},{129,1},{193,65... | collective-permute-start | bytes 49160 | tf_op jit(solution)/shard_map/ppermute | solution.py:45
  54.5 0.8 collective-permute-start.11
  55.3 0.7 collective-permute-start.10
  56.0 1.2 copy-done.4
  57.2 2.4 %shard_map.123.total_ref = f32[512,1024]{1,0:T(8,128)S(1)} custom-call(bf16[8,2048]{1,0:T(8,128)(2,1)S(1)} %slice.170.after, bf16[256,1024]{1,0:T(8,128)(2,1)S(1)} %get-tuple-element.26.roles, bf16[256,256]{1,0:T(8,128)(2,1)S(1)} %get-tuple-element.27.local, bf16[2,256,1024]{2,1,0:T(8,128)(2,1)S(1)} %copy-done.2, bf16[512,1024]{1,0:T(8,128)(2,1)S(1)} %copy-done.4, ...), custom_call_target="tpu_custom_call" | custom-call | flops 805306368 | bytes 6455296 | tf_op jit(solution)/shard_map/pallas_call | solution.py:108
  59.7 0.8 shard_map.124
  60.9 3.0 %fusion.2 = (bf16[512,1024]{1,0:T(8,128)(2,1)S(1)}, bf16[512,1024]{1,0:T(8,128)(2,1)}) fusion(bf16[2,256,1024]{2,1,0:T(8,128)(2,1)S(1)} %copy-done.12, bf16[512,1024]{1,0:T(8,128)(2,1)S(1)} %shard_map.124, bf16[1024,1024]{1,0:T(8,128)(2,1)S(1)} %copy-done), kind=kOutput, calls=%fused_computation.4 | convolution fusion | flops 1080033280 | bytes 6291456 | tf_op jit(solution)/shard_map/dot_general | solution.py:75
  63.9 1.3 convolution_convert_fusion
  65.1 0.7 convolution_convert_fusion.2
  65.9 1.7 %collective-permute-start.26 = (bf16[512,1024]{1,0:T(8,128)(2,1)S(1)}, bf16[512,1024]{1,0:T(8,128)(2,1)S(1)}, u32[]{:S(2)}, u32[]{:S(2)}) collective-permute-start(bf16[512,1024]{1,0:T(8,128)(2,1)S(1)} %convolution_convert_fusion.2), channel_id=1, source_target_pairs={{0,1},{1,0},{2,3},{3,2},{4,5},{5,4},{6,7},{7,6},{8,9},{9,8},{10,11... | collective-permute-start | bytes 3145736 | tf_op jit(solution)/shard_map/ppermute | solution.py:33
  67.6 1.2 convolution_convert_fusion.1.dagg_ref
  68.9 1.1 shard_map.126
  70.0 0.5 collective-permute-start.18
  70.5 2.3 %collective-permute-start.17 = (bf16[4,2048]{1,0:T(4,128)(2,1)S(1)}, bf16[4,2048]{1,0:T(4,128)(2,1)S(1)}, u32[]{:S(2)}, u32[]{:S(2)}) collective-permute-start(bf16[4,2048]{1,0:T(4,128)(2,1)S(1)} %get-tuple-element.34), channel_id=1, source_target_pairs={{0,192},{64,0},{128,64},{192,128},{1,193},{65,1},{129,65},{193,129... | collective-permute-start | bytes 49160 | tf_op jit(solution)/shard_map/ppermute | solution.py:45
  72.9 0.7 fusion.5
  73.6 0.7 shard_map.125
  74.3 0.7 collective-permute-start.13
  75.0 0.5 fusion.24
  75.6 1.6 %collective-permute-start.27 = (bf16[64,1024]{1,0:T(8,128)(2,1)S(1)}, bf16[64,1024]{1,0:T(8,128)(2,1)S(1)}, u32[]{:S(2)}, u32[]{:S(2)}) collective-permute-start(bf16[64,1024]{1,0:T(8,128)(2,1)S(1)} %get-tuple-element.46), channel_id=1, source_target_pairs={{0,64},{64,128},{128,192},{192,0},{1,65},{65,129},{129,193},{193,1... | collective-permute-start | bytes 393224 | tf_op jit(solution)/shard_map/ppermute | solution.py:45
  77.2 1.7 %collective-permute-start.29 = (bf16[64,1024]{1,0:T(8,128)(2,1)S(1)}, bf16[64,1024]{1,0:T(8,128)(2,1)S(1)}, u32[]{:S(2)}, u32[]{:S(2)}) collective-permute-start(bf16[64,1024]{1,0:T(8,128)(2,1)S(1)} %get-tuple-element.47), channel_id=1, source_target_pairs={{0,192},{64,0},{128,64},{192,128},{1,193},{65,1},{129,65},{193,129... | collective-permute-start | bytes 393224 | tf_op jit(solution)/shard_map/ppermute | solution.py:45
  79.0 3.2 %collective-permute-start.19 = (bf16[4,2048]{1,0:T(4,128)(2,1)S(1)}, bf16[4,2048]{1,0:T(4,128)(2,1)S(1)}, u32[]{:S(2)}, u32[]{:S(2)}) collective-permute-start(bf16[4,2048]{1,0:T(4,128)(2,1)S(1)} %add_convert_fusion), channel_id=1, source_target_pairs={{0,8},{1,9},{2,10},{3,11},{4,12},{5,13},{6,14},{7,15},{8,0},{9,1},... | collective-permute-start | bytes 49160 | tf_op jit(solution)/shard_map/ppermute | solution.py:41
  82.6 2.8 %collective-permute-start.30 = (bf16[128,1024]{1,0:T(8,128)(2,1)S(1)}, bf16[128,1024]{1,0:T(8,128)(2,1)S(1)}, u32[]{:S(2)}, u32[]{:S(2)}) collective-permute-start(bf16[128,1024]{1,0:T(8,128)(2,1)S(1)} %pad_maximum_fusion.1), channel_id=1, source_target_pairs={{0,192},{64,0},{128,64},{192,128},{1,193},{65,1},{129,65},{193,129... | collective-permute-start | bytes 786440 | tf_op jit(solution)/shard_map/ppermute | solution.py:45
  85.6 0.5 collective-permute-start.20
  86.1 2.8 %collective-permute-start.14 = (bf16[512,1024]{1,0:T(8,128)(2,1)S(1)}, bf16[512,1024]{1,0:T(8,128)(2,1)S(1)}, u32[]{:S(2)}, u32[]{:S(2)}) collective-permute-start(bf16[512,1024]{1,0:T(8,128)(2,1)S(1)} %get-tuple-element.31), channel_id=1, source_target_pairs={{1,3},{2,0},{3,5},{4,2},{5,7},{6,4},{7,9},{8,6},{9,11},{10,8},{11,... | collective-permute-start | bytes 3145736 | tf_op jit(solution)/shard_map/ppermute | solution.py:55
  89.3 1.0 collective-permute-start.21
  90.3 3.0 %collective-permute-done.28 = bf16[128,1024]{1,0:T(8,128)(2,1)S(1)} collective-permute-done((bf16[128,1024]{1,0:T(8,128)(2,1)S(1)}, bf16[128,1024]{1,0:T(8,128)(2,1)S(1)}, u32[]{:S(2)}, u32[]{:S(2)}) %collective-permute-start.28) | collective-permute-done | bytes 262176 | tf_op jit(solution)/shard_map/ppermute | solution.py:45
  93.9 1.8 %collective-permute-start.33 = (bf16[32,1024]{1,0:T(8,128)(2,1)S(1)}, bf16[32,1024]{1,0:T(8,128)(2,1)S(1)}, u32[]{:S(2)}, u32[]{:S(2)}) collective-permute-start(bf16[32,1024]{1,0:T(8,128)(2,1)S(1)} %get-tuple-element.51), channel_id=1, source_target_pairs={{0,32},{1,33},{2,34},{3,35},{4,36},{5,37},{6,38},{7,39},{8,40},{9,... | collective-permute-start | bytes 196616 | tf_op jit(solution)/shard_map/ppermute | solution.py:37
  95.6 1.1 collective-permute-start.32
  96.7 0.4 shard_map.127
  97.1 4.9 %collective-permute-done.21 = bf16[16,2048]{1,0:T(8,128)(2,1)S(1)} collective-permute-done((bf16[16,2048]{1,0:T(8,128)(2,1)S(1)}, bf16[16,2048]{1,0:T(8,128)(2,1)S(1)}, u32[]{:S(2)}, u32[]{:S(2)}) %collective-permute-start.21) | collective-permute-done | bytes 65568 | tf_op jit(solution)/shard_map/ppermute | solution.py:41
  102.0 1.3 collective-permute-start.15
  103.3 0.9 collective-permute-done.31
  104.2 4.5 %collective-permute-start.24 = (bf16[32,2048]{1,0:T(8,128)(2,1)S(1)}, bf16[32,2048]{1,0:T(8,128)(2,1)S(1)}, u32[]{:S(2)}, u32[]{:S(2)}) collective-permute-start(bf16[32,2048]{1,0:T(8,128)(2,1)S(1)} %pad_maximum_fusion.2.own_ref), channel_id=1, source_target_pairs={{0,16},{1,17},{2,18},{3,19},{4,20},{5,21},{6,22},{7,23},{8,24},{9,... | collective-permute-start | bytes 393224 | tf_op jit(solution)/shard_map/ppermute | solution.py:37
  108.7 0.9 collective-permute-start.23
  109.6 2.0 %collective-permute-start.22 = (bf16[32,2048]{1,0:T(8,128)(2,1)S(1)}, bf16[32,2048]{1,0:T(8,128)(2,1)S(1)}, u32[]{:S(2)}, u32[]{:S(2)}) collective-permute-start(bf16[32,2048]{1,0:T(8,128)(2,1)S(1)} %pad_maximum_fusion.2.own_ref), channel_id=1, source_target_pairs={{0,48},{1,49},{2,50},{3,51},{4,52},{5,53},{6,54},{7,55},{8,56},{9,... | collective-permute-start | bytes 393224 | tf_op jit(solution)/shard_map/ppermute | solution.py:37
  111.7 11.4 %collective-permute-done.24.three_ref = bf16[32,2048]{1,0:T(8,128)(2,1)S(1)} collective-permute-done((bf16[32,2048]{1,0:T(8,128)(2,1)S(1)}, bf16[32,2048]{1,0:T(8,128)(2,1)S(1)}, u32[]{:S(2)}, u32[]{:S(2)}) %collective-permute-start.24) | collective-permute-done | bytes 131104 | tf_op jit(solution)/shard_map/ppermute | solution.py:37
  123.1 3.9 %collective-permute-done.23.two_ref = bf16[32,2048]{1,0:T(8,128)(2,1)S(1)} collective-permute-done((bf16[32,2048]{1,0:T(8,128)(2,1)S(1)}, bf16[32,2048]{1,0:T(8,128)(2,1)S(1)}, u32[]{:S(2)}, u32[]{:S(2)}) %collective-permute-start.23) | collective-permute-done | bytes 131104 | tf_op jit(solution)/shard_map/ppermute | solution.py:37
  127.0 1.2 collective-permute-start.25
  128.3 3.5 %collective-permute-done.35 = bf16[8,1024]{1,0:T(8,128)(2,1)S(1)} collective-permute-done((bf16[8,1024]{1,0:T(8,128)(2,1)S(1)}, bf16[8,1024]{1,0:T(8,128)(2,1)S(1)}, u32[]{:S(2)}, u32[]{:S(2)}) %collective-permute-start.35) | collective-permute-done | bytes 16416 | tf_op jit(solution)/shard_map/ppermute | solution.py:41
  131.9 6.4 %collective-permute-done.36 = bf16[4,1024]{1,0:T(4,128)(2,1)S(1)} collective-permute-done((bf16[4,1024]{1,0:T(4,128)(2,1)S(1)}, bf16[4,1024]{1,0:T(4,128)(2,1)S(1)}, u32[]{:S(2)}, u32[]{:S(2)}) %collective-permute-start.36) | collective-permute-done | bytes 8224 | tf_op jit(solution)/shard_map/ppermute | solution.py:41
  138.3 0.6 fusion.9
  138.9 1.6 %shard_map.128 = (f32[512,1024]{1,0:T(8,128)S(1)}, bf16[256,1024]{1,0:T(8,128)(2,1)}) custom-call(bf16[256,256]{1,0:T(8,128)(2,1)S(1)} %get-tuple-element.29.local_t, bf16[512,1024]{1,0:T(8,128)(2,1)S(1)} %convolution_convert_fusion.1.dagg_ref, bf16[1024,1024]{1,0:T(8,128)(2,1)S(1)} %collective-permute-done.13.got_ref.pair_ref, ...), custom_call_target="tpu_custom_call" | custom-call | flops 268435456 | bytes 7995392 | tf_op jit(solution)/shard_map/pallas_call | solution.py:108
  140.5 1.7 %shard_map.130 = bf16[2,256,1024]{2,1,0:T(8,128)(2,1)} custom-call(f32[512,1024]{1,0:T(8,128)S(1)} %get-tuple-element.32.base_ref, bf16[256,256]{1,0:T(8,128)(2,1)S(1)} %get-tuple-element.33.rel_t, bf16[128,2048]{1,0:T(8,128)(2,1)S(1)} %shard_map.129.own_ref, bf16[128,2048]{1,0:T(8,128)(2,1)S(1)} %collective-permute-done.25.got_ref), custom_call_target="tpu_custom_call" | custom-call | flops 268435456 | bytes 4325376 | tf_op jit(solution)/shard_map/pallas_call | solution.py:108
  (81 shorter events, 3.1 us)
Async XLA Ops:
  0.6 59.8 %copy-start = (bf16[1024,1024]{1,0:T(8,128)(2,1)S(1)}, bf16[1024,1024]{1,0:T(8,128)(2,1)}, u32[]{:S(2)}) copy-start(bf16[1024,1024]{1,0:T(8,128)(2,1)} %param.16) | copy-start | bytes 6291460
  0.6 1.4 copy-start.1
  2.0 0.9 copy-start.6
  4.3 5.5 %collective-permute-start = (bf16[512,1024]{1,0:T(8,128)(2,1)S(1)}, bf16[512,1024]{1,0:T(8,128)(2,1)S(1)}, u32[]{:S(2)}, u32[]{:S(2)}) collective-permute-start(bf16[512,1024]{1,0:T(8,128)(2,1)S(1)} %get-tuple-element.20), channel_id=1, source_target_pairs={{0,1},{1,0},{2,3},{3,2},{4,5},{5,4},{6,7},{7,6},{8,9},{9,8},{10,11... | collective-permute-start | bytes 3145736 | tf_op jit(solution)/shard_map/ppermute | solution.py:33
  9.8 8.5 %copy-start.3 = (bf16[512,1024]{1,0:T(8,128)(2,1)}, bf16[512,1024]{1,0:T(8,128)(2,1)S(1)}, u32[]{:S(2)}) copy-start(bf16[512,1024]{1,0:T(8,128)(2,1)S(1)} %collective-permute-done.got_ref.pair_ref) | copy-start | bytes 3145732
  9.9 39.2 %copy-start.11 = (s32[1,64,4,2]{1,3,2,0:T(2,128)S(1)}, s32[1,64,4,2]{1,3,2,0:T(2,128)}, u32[]{:S(2)}) copy-start(s32[1,64,4,2]{1,3,2,0:T(2,128)} %param.13) | copy-start | bytes 6148
  9.9 39.5 %copy-start.7 = (bf16[256,256]{1,0:T(8,128)(2,1)S(1)}, bf16[256,256]{1,0:T(8,128)(2,1)}, u32[]{:S(2)}) copy-start(bf16[256,256]{1,0:T(8,128)(2,1)} %a_ref.1) | copy-start | bytes 393220
  9.9 39.5 %copy-start.9 = (s32[2,2]{1,0:T(2,128)S(1)}, s32[2,2]{1,0:T(2,128)}, u32[]{:S(2)}) copy-start(s32[2,2]{1,0:T(2,128)} %present.1) | copy-start | bytes 52
  9.9 6.0 %collective-permute-start.1 = (bf16[32,2048]{1,0:T(8,128)(2,1)S(1)}, bf16[32,2048]{1,0:T(8,128)(2,1)S(1)}, u32[]{:S(2)}, u32[]{:S(2)}) collective-permute-start(bf16[32,2048]{1,0:T(8,128)(2,1)S(1)} %get-tuple-element.23), channel_id=1, source_target_pairs={{0,16},{1,17},{2,18},{3,19},{4,20},{5,21},{6,22},{7,23},{8,24},{9,... | collective-permute-start | bytes 393224 | tf_op jit(solution)/shard_map/ppermute | solution.py:37
  10.0 7.8 %collective-permute-start.2 = (bf16[32,2048]{1,0:T(8,128)(2,1)S(1)}, bf16[32,2048]{1,0:T(8,128)(2,1)S(1)}, u32[]{:S(2)}, u32[]{:S(2)}) collective-permute-start(bf16[32,2048]{1,0:T(8,128)(2,1)S(1)} %get-tuple-element.24), channel_id=1, source_target_pairs={{0,48},{1,49},{2,50},{3,51},{4,52},{5,53},{6,54},{7,55},{8,56},{9,... | collective-permute-start | bytes 393224 | tf_op jit(solution)/shard_map/ppermute | solution.py:37
  12.7 5.6 %collective-permute-start.3 = (bf16[32,2048]{1,0:T(8,128)(2,1)S(1)}, bf16[32,2048]{1,0:T(8,128)(2,1)S(1)}, u32[]{:S(2)}, u32[]{:S(2)}) collective-permute-start(bf16[32,2048]{1,0:T(8,128)(2,1)S(1)} %get-tuple-element.25), channel_id=1, source_target_pairs={{0,32},{1,33},{2,34},{3,35},{4,36},{5,37},{6,38},{7,39},{8,40},{9,... | collective-permute-start | bytes 393224 | tf_op jit(solution)/shard_map/ppermute | solution.py:37
  18.3 37.7 %copy-start.2 = (bf16[2,256,1024]{2,1,0:T(8,128)(2,1)S(1)}, bf16[2,256,1024]{2,1,0:T(8,128)(2,1)}, u32[]{:S(2)}) copy-start(bf16[2,256,1024]{2,1,0:T(8,128)(2,1)} %f_ref.3) | copy-start | bytes 3145732
  20.6 7.4 %collective-permute-start.4 = (bf16[16,2048]{1,0:T(8,128)(2,1)}, bf16[16,2048]{1,0:T(8,128)(2,1)S(1)}, u32[]{:S(2)}, u32[]{:S(2)}) collective-permute-start(bf16[16,2048]{1,0:T(8,128)(2,1)} %slice.168), channel_id=1, source_target_pairs={{0,2},{1,3},{2,0},{3,1},{4,6},{5,7},{6,4},{7,5},{8,10},{9,11},{10,... | collective-permute-start | bytes 196616 | tf_op jit(solution)/shard_map/ppermute | solution.py:41
  21.9 34.1 %collective-permute-start.7 = (bf16[256,1024]{1,0:T(8,128)(2,1)}, bf16[256,1024]{1,0:T(8,128)(2,1)}, u32[]{:S(2)}, u32[]{:S(2)}) collective-permute-start(bf16[256,1024]{1,0:T(8,128)(2,1)} %get-tuple-element.28), channel_id=1, source_target_pairs={{0,2},{2,4},{3,1},{4,6},{5,3},{6,8},{7,5},{8,10},{9,7},{10,12},{11... | collective-permute-start | bytes 1572872 | tf_op jit(solution)/shard_map/ppermute | solution.py:55
  23.2 15.7 %collective-permute-start.5 = (bf16[256,1024]{1,0:T(8,128)(2,1)}, bf16[256,1024]{1,0:T(8,128)(2,1)}, u32[]{:S(2)}, u32[]{:S(2)}) collective-permute-start(bf16[256,1024]{1,0:T(8,128)(2,1)} %get-tuple-element.28), channel_id=1, source_target_pairs={{1,3},{2,0},{3,5},{4,2},{5,7},{6,4},{7,9},{8,6},{9,11},{10,8},{11,... | collective-permute-start | bytes 1572872 | tf_op jit(solution)/shard_map/ppermute | solution.py:55
  28.9 10.2 %collective-permute-start.8 = (bf16[8,2048]{1,0:T(8,128)(2,1)S(1)}, bf16[8,2048]{1,0:T(8,128)(2,1)S(1)}, u32[]{:S(2)}, u32[]{:S(2)}) collective-permute-start(bf16[8,2048]{1,0:T(8,128)(2,1)S(1)} %slice.170.after), channel_id=1, source_target_pairs={{0,4},{1,5},{2,6},{3,7},{4,0},{5,1},{6,2},{7,3},{8,12},{9,13},{10,... | collective-permute-start | bytes 98312 | tf_op jit(solution)/shard_map/ppermute | solution.py:41
  38.9 17.1 %collective-permute-start.6 = (bf16[256,1024]{1,0:T(8,128)(2,1)}, bf16[256,1024]{1,0:T(8,128)(2,1)}, u32[]{:S(2)}, u32[]{:S(2)}) collective-permute-start(bf16[256,1024]{1,0:T(8,128)(2,1)} %collective-permute-done.5.first_ref), channel_id=1, source_target_pairs={{0,1},{1,0},{2,3},{3,2},{4,5},{5,4},{6,7},{7,6},{8,9},{9,8},{10,11... | collective-permute-start | bytes 1572872 | tf_op jit(solution)/shard_map/ppermute | solution.py:33
  39.2 12.3 %collective-permute-start.9 = (bf16[4,2048]{1,0:T(4,128)(2,1)S(1)}, bf16[4,2048]{1,0:T(4,128)(2,1)S(1)}, u32[]{:S(2)}, u32[]{:S(2)}) collective-permute-start(bf16[4,2048]{1,0:T(4,128)(2,1)S(1)} %slice.172), channel_id=1, source_target_pairs={{0,8},{1,9},{2,10},{3,11},{4,12},{5,13},{6,14},{7,15},{8,0},{9,1},... | collective-permute-start | bytes 49160 | tf_op jit(solution)/shard_map/ppermute | solution.py:41
  49.4 1.1 copy-start.5
  51.5 8.1 %collective-permute-start.12 = (bf16[4,2048]{1,0:T(4,128)(2,1)S(1)}, bf16[4,2048]{1,0:T(4,128)(2,1)S(1)}, u32[]{:S(2)}, u32[]{:S(2)}) collective-permute-start(bf16[4,2048]{1,0:T(4,128)(2,1)S(1)} %get-tuple-element.40), channel_id=1, source_target_pairs={{0,128},{64,192},{128,0},{192,64},{1,129},{65,193},{129,1},{193,65... | collective-permute-start | bytes 49160 | tf_op jit(solution)/shard_map/ppermute | solution.py:45
  54.5 5.2 %collective-permute-start.11 = (bf16[4,2048]{1,0:T(4,128)(2,1)S(1)}, bf16[4,2048]{1,0:T(4,128)(2,1)S(1)}, u32[]{:S(2)}, u32[]{:S(2)}) collective-permute-start(bf16[4,2048]{1,0:T(4,128)(2,1)S(1)} %get-tuple-element.40), channel_id=1, source_target_pairs={{0,192},{64,0},{128,64},{192,128},{1,193},{65,1},{129,65},{193,129... | collective-permute-start | bytes 49160 | tf_op jit(solution)/shard_map/ppermute | solution.py:45
  55.3 4.4 %collective-permute-start.10 = (bf16[4,2048]{1,0:T(4,128)(2,1)S(1)}, bf16[4,2048]{1,0:T(4,128)(2,1)S(1)}, u32[]{:S(2)}, u32[]{:S(2)}) collective-permute-start(bf16[4,2048]{1,0:T(4,128)(2,1)S(1)} %get-tuple-element.40), channel_id=1, source_target_pairs={{0,64},{64,128},{128,192},{192,0},{1,65},{65,129},{129,193},{193,1... | collective-permute-start | bytes 49160 | tf_op jit(solution)/shard_map/ppermute | solution.py:45
  56.0 1.2 copy-start.4
  57.2 2.5 %copy-start.8 = (s32[1,4]{1,0:T(1,128)S(1)}, s32[1,4]{1,0:T(1,128)}, u32[]{:S(2)}) copy-start(s32[1,4]{1,0:T(1,128)} %offs.3) | copy-start | bytes 52
  59.7 1.2 copy-start.12
  60.9 3.0 %copy-start.10 = (bf16[1024,1024]{1,0:T(8,128)(2,1)S(1)}, bf16[1024,1024]{1,0:T(8,128)(2,1)}, u32[]{:S(2)}) copy-start(bf16[1024,1024]{1,0:T(8,128)(2,1)} %fusion) | copy-start | bytes 6291460
  65.9 9.1 %collective-permute-start.26 = (bf16[512,1024]{1,0:T(8,128)(2,1)S(1)}, bf16[512,1024]{1,0:T(8,128)(2,1)S(1)}, u32[]{:S(2)}, u32[]{:S(2)}) collective-permute-start(bf16[512,1024]{1,0:T(8,128)(2,1)S(1)} %convolution_convert_fusion.2), channel_id=1, source_target_pairs={{0,1},{1,0},{2,3},{3,2},{4,5},{5,4},{6,7},{7,6},{8,9},{9,8},{10,11... | collective-permute-start | bytes 3145736 | tf_op jit(solution)/shard_map/ppermute | solution.py:33
  70.0 7.2 %collective-permute-start.18 = (bf16[4,2048]{1,0:T(4,128)(2,1)S(1)}, bf16[4,2048]{1,0:T(4,128)(2,1)S(1)}, u32[]{:S(2)}, u32[]{:S(2)}) collective-permute-start(bf16[4,2048]{1,0:T(4,128)(2,1)S(1)} %get-tuple-element.34), channel_id=1, source_target_pairs={{0,128},{64,192},{128,0},{192,64},{1,129},{65,193},{129,1},{193,65... | collective-permute-start | bytes 49160 | tf_op jit(solution)/shard_map/ppermute | solution.py:45
  70.5 8.4 %collective-permute-start.17 = (bf16[4,2048]{1,0:T(4,128)(2,1)S(1)}, bf16[4,2048]{1,0:T(4,128)(2,1)S(1)}, u32[]{:S(2)}, u32[]{:S(2)}) collective-permute-start(bf16[4,2048]{1,0:T(4,128)(2,1)S(1)} %get-tuple-element.34), channel_id=1, source_target_pairs={{0,192},{64,0},{128,64},{192,128},{1,193},{65,1},{129,65},{193,129... | collective-permute-start | bytes 49160 | tf_op jit(solution)/shard_map/ppermute | solution.py:45
  72.9 6.1 %collective-permute-start.16 = (bf16[4,2048]{1,0:T(4,128)(2,1)S(1)}, bf16[4,2048]{1,0:T(4,128)(2,1)S(1)}, u32[]{:S(2)}, u32[]{:S(2)}) collective-permute-start(bf16[4,2048]{1,0:T(4,128)(2,1)S(1)} %get-tuple-element.34), channel_id=1, source_target_pairs={{0,64},{64,128},{128,192},{192,0},{1,65},{65,129},{129,193},{193,1... | collective-permute-start | bytes 49160 | tf_op jit(solution)/shard_map/ppermute | solution.py:45
  74.3 21.3 %collective-permute-start.13 = (bf16[1024,1024]{1,0:T(8,128)(2,1)S(1)}, bf16[1024,1024]{1,0:T(8,128)(2,1)S(1)}, u32[]{:S(2)}, u32[]{:S(2)}) collective-permute-start(bf16[1024,1024]{1,0:T(8,128)(2,1)S(1)} %shard_map.125), channel_id=1, source_target_pairs={{0,1},{1,0},{2,3},{3,2},{4,5},{5,4},{6,7},{7,6},{8,9},{9,8},{10,11... | collective-permute-start | bytes 6291464 | tf_op jit(solution)/shard_map/ppermute | solution.py:33
  75.6 6.9 %collective-permute-start.27 = (bf16[64,1024]{1,0:T(8,128)(2,1)S(1)}, bf16[64,1024]{1,0:T(8,128)(2,1)S(1)}, u32[]{:S(2)}, u32[]{:S(2)}) collective-permute-start(bf16[64,1024]{1,0:T(8,128)(2,1)S(1)} %get-tuple-element.46), channel_id=1, source_target_pairs={{0,64},{64,128},{128,192},{192,0},{1,65},{65,129},{129,193},{193,1... | collective-permute-start | bytes 393224 | tf_op jit(solution)/shard_map/ppermute | solution.py:45
  77.2 5.3 %collective-permute-start.29 = (bf16[64,1024]{1,0:T(8,128)(2,1)S(1)}, bf16[64,1024]{1,0:T(8,128)(2,1)S(1)}, u32[]{:S(2)}, u32[]{:S(2)}) collective-permute-start(bf16[64,1024]{1,0:T(8,128)(2,1)S(1)} %get-tuple-element.47), channel_id=1, source_target_pairs={{0,192},{64,0},{128,64},{192,128},{1,193},{65,1},{129,65},{193,129... | collective-permute-start | bytes 393224 | tf_op jit(solution)/shard_map/ppermute | solution.py:45
  79.0 6.6 %collective-permute-start.19 = (bf16[4,2048]{1,0:T(4,128)(2,1)S(1)}, bf16[4,2048]{1,0:T(4,128)(2,1)S(1)}, u32[]{:S(2)}, u32[]{:S(2)}) collective-permute-start(bf16[4,2048]{1,0:T(4,128)(2,1)S(1)} %add_convert_fusion), channel_id=1, source_target_pairs={{0,8},{1,9},{2,10},{3,11},{4,12},{5,13},{6,14},{7,15},{8,0},{9,1},... | collective-permute-start | bytes 49160 | tf_op jit(solution)/shard_map/ppermute | solution.py:41
  82.6 7.8 %collective-permute-start.30 = (bf16[128,1024]{1,0:T(8,128)(2,1)S(1)}, bf16[128,1024]{1,0:T(8,128)(2,1)S(1)}, u32[]{:S(2)}, u32[]{:S(2)}) collective-permute-start(bf16[128,1024]{1,0:T(8,128)(2,1)S(1)} %pad_maximum_fusion.1), channel_id=1, source_target_pairs={{0,192},{64,0},{128,64},{192,128},{1,193},{65,1},{129,65},{193,129... | collective-permute-start | bytes 786440 | tf_op jit(solution)/shard_map/ppermute | solution.py:45
  85.4 8.0 %collective-permute-start.28 = (bf16[128,1024]{1,0:T(8,128)(2,1)S(1)}, bf16[128,1024]{1,0:T(8,128)(2,1)S(1)}, u32[]{:S(2)}, u32[]{:S(2)}) collective-permute-start(bf16[128,1024]{1,0:T(8,128)(2,1)S(1)} %pad_maximum_fusion), channel_id=1, source_target_pairs={{0,64},{64,128},{128,192},{192,0},{1,65},{65,129},{129,193},{193,1... | collective-permute-start | bytes 786440 | tf_op jit(solution)/shard_map/ppermute | solution.py:45
  85.6 3.8 %collective-permute-start.20 = (bf16[8,2048]{1,0:T(8,128)(2,1)S(1)}, bf16[8,2048]{1,0:T(8,128)(2,1)S(1)}, u32[]{:S(2)}, u32[]{:S(2)}) collective-permute-start(bf16[8,2048]{1,0:T(8,128)(2,1)S(1)} %pad_maximum_fusion.4), channel_id=1, source_target_pairs={{0,4},{1,5},{2,6},{3,7},{4,0},{5,1},{6,2},{7,3},{8,12},{9,13},{10,... | collective-permute-start | bytes 98312 | tf_op jit(solution)/shard_map/ppermute | solution.py:41
  86.1 52.8 %collective-permute-start.14 = (bf16[512,1024]{1,0:T(8,128)(2,1)S(1)}, bf16[512,1024]{1,0:T(8,128)(2,1)S(1)}, u32[]{:S(2)}, u32[]{:S(2)}) collective-permute-start(bf16[512,1024]{1,0:T(8,128)(2,1)S(1)} %get-tuple-element.31), channel_id=1, source_target_pairs={{1,3},{2,0},{3,5},{4,2},{5,7},{6,4},{7,9},{8,6},{9,11},{10,8},{11,... | collective-permute-start | bytes 3145736 | tf_op jit(solution)/shard_map/ppermute | solution.py:55
  89.3 12.7 %collective-permute-start.21 = (bf16[16,2048]{1,0:T(8,128)(2,1)S(1)}, bf16[16,2048]{1,0:T(8,128)(2,1)S(1)}, u32[]{:S(2)}, u32[]{:S(2)}) collective-permute-start(bf16[16,2048]{1,0:T(8,128)(2,1)S(1)} %pad_maximum_fusion.3), channel_id=1, source_target_pairs={{0,2},{1,3},{2,0},{3,1},{4,6},{5,7},{6,4},{7,5},{8,10},{9,11},{10,... | collective-permute-start | bytes 196616 | tf_op jit(solution)/shard_map/ppermute | solution.py:41
  93.5 10.7 %collective-permute-start.31 = (bf16[32,1024]{1,0:T(8,128)(2,1)S(1)}, bf16[32,1024]{1,0:T(8,128)(2,1)S(1)}, u32[]{:S(2)}, u32[]{:S(2)}) collective-permute-start(bf16[32,1024]{1,0:T(8,128)(2,1)S(1)} %get-tuple-element.50), channel_id=1, source_target_pairs={{0,16},{1,17},{2,18},{3,19},{4,20},{5,21},{6,22},{7,23},{8,24},{9,... | collective-permute-start | bytes 196616 | tf_op jit(solution)/shard_map/ppermute | solution.py:37
  93.9 14.8 %collective-permute-start.33 = (bf16[32,1024]{1,0:T(8,128)(2,1)S(1)}, bf16[32,1024]{1,0:T(8,128)(2,1)S(1)}, u32[]{:S(2)}, u32[]{:S(2)}) collective-permute-start(bf16[32,1024]{1,0:T(8,128)(2,1)S(1)} %get-tuple-element.51), channel_id=1, source_target_pairs={{0,32},{1,33},{2,34},{3,35},{4,36},{5,37},{6,38},{7,39},{8,40},{9,... | collective-permute-start | bytes 196616 | tf_op jit(solution)/shard_map/ppermute | solution.py:37
  95.6 14.0 %collective-permute-start.32 = (bf16[32,1024]{1,0:T(8,128)(2,1)S(1)}, bf16[32,1024]{1,0:T(8,128)(2,1)S(1)}, u32[]{:S(2)}, u32[]{:S(2)}) collective-permute-start(bf16[32,1024]{1,0:T(8,128)(2,1)S(1)} %get-tuple-element.52), channel_id=1, source_target_pairs={{0,48},{1,49},{2,50},{3,51},{4,52},{5,53},{6,54},{7,55},{8,56},{9,... | collective-permute-start | bytes 196616 | tf_op jit(solution)/shard_map/ppermute | solution.py:37
  102.0 36.9 %collective-permute-start.15 = (bf16[512,1024]{1,0:T(8,128)(2,1)S(1)}, bf16[512,1024]{1,0:T(8,128)(2,1)S(1)}, u32[]{:S(2)}, u32[]{:S(2)}) collective-permute-start(bf16[512,1024]{1,0:T(8,128)(2,1)S(1)} %shard_map.127), channel_id=1, source_target_pairs={{0,2},{2,4},{3,1},{4,6},{5,3},{6,8},{7,5},{8,10},{9,7},{10,12},{11... | collective-permute-start | bytes 3145736 | tf_op jit(solution)/shard_map/ppermute | solution.py:55
  104.2 18.9 %collective-permute-start.24 = (bf16[32,2048]{1,0:T(8,128)(2,1)S(1)}, bf16[32,2048]{1,0:T(8,128)(2,1)S(1)}, u32[]{:S(2)}, u32[]{:S(2)}) collective-permute-start(bf16[32,2048]{1,0:T(8,128)(2,1)S(1)} %pad_maximum_fusion.2.own_ref), channel_id=1, source_target_pairs={{0,16},{1,17},{2,18},{3,19},{4,20},{5,21},{6,22},{7,23},{8,24},{9,... | collective-permute-start | bytes 393224 | tf_op jit(solution)/shard_map/ppermute | solution.py:37
  108.7 18.3 %collective-permute-start.23 = (bf16[32,2048]{1,0:T(8,128)(2,1)S(1)}, bf16[32,2048]{1,0:T(8,128)(2,1)S(1)}, u32[]{:S(2)}, u32[]{:S(2)}) collective-permute-start(bf16[32,2048]{1,0:T(8,128)(2,1)S(1)} %pad_maximum_fusion.2.own_ref), channel_id=1, source_target_pairs={{0,32},{1,33},{2,34},{3,35},{4,36},{5,37},{6,38},{7,39},{8,40},{9,... | collective-permute-start | bytes 393224 | tf_op jit(solution)/shard_map/ppermute | solution.py:37
  109.6 17.3 %collective-permute-start.22 = (bf16[32,2048]{1,0:T(8,128)(2,1)S(1)}, bf16[32,2048]{1,0:T(8,128)(2,1)S(1)}, u32[]{:S(2)}, u32[]{:S(2)}) collective-permute-start(bf16[32,2048]{1,0:T(8,128)(2,1)S(1)} %pad_maximum_fusion.2.own_ref), channel_id=1, source_target_pairs={{0,48},{1,49},{2,50},{3,51},{4,52},{5,53},{6,54},{7,55},{8,56},{9,... | collective-permute-start | bytes 393224 | tf_op jit(solution)/shard_map/ppermute | solution.py:37
  123.1 5.1 %collective-permute-start.34 = (bf16[16,1024]{1,0:T(8,128)(2,1)S(1)}, bf16[16,1024]{1,0:T(8,128)(2,1)S(1)}, u32[]{:S(2)}, u32[]{:S(2)}) collective-permute-start(bf16[16,1024]{1,0:T(8,128)(2,1)S(1)} %slice.169), channel_id=1, source_target_pairs={{0,2},{1,3},{2,0},{3,1},{4,6},{5,7},{6,4},{7,5},{8,10},{9,11},{10,... | collective-permute-start | bytes 98312 | tf_op jit(solution)/shard_map/ppermute | solution.py:41
  127.0 13.5 %collective-permute-start.25 = (bf16[128,2048]{1,0:T(8,128)(2,1)S(1)}, bf16[128,2048]{1,0:T(8,128)(2,1)S(1)}, u32[]{:S(2)}, u32[]{:S(2)}) collective-permute-start(bf16[128,2048]{1,0:T(8,128)(2,1)S(1)} %shard_map.129.own_ref), channel_id=1, source_target_pairs={{0,1},{1,0},{2,3},{3,2},{4,5},{5,4},{6,7},{7,6},{8,9},{9,8},{10,11... | collective-permute-start | bytes 1572872 | tf_op jit(solution)/shard_map/ppermute | solution.py:33
  128.2 3.6 %collective-permute-start.35 = (bf16[8,1024]{1,0:T(8,128)(2,1)S(1)}, bf16[8,1024]{1,0:T(8,128)(2,1)S(1)}, u32[]{:S(2)}, u32[]{:S(2)}) collective-permute-start(bf16[8,1024]{1,0:T(8,128)(2,1)S(1)} %slice.171), channel_id=1, source_target_pairs={{0,4},{1,5},{2,6},{3,7},{4,0},{5,1},{6,2},{7,3},{8,12},{9,13},{10,... | collective-permute-start | bytes 49160 | tf_op jit(solution)/shard_map/ppermute | solution.py:41
  131.8 6.5 %collective-permute-start.36 = (bf16[4,1024]{1,0:T(4,128)(2,1)S(1)}, bf16[4,1024]{1,0:T(4,128)(2,1)S(1)}, u32[]{:S(2)}, u32[]{:S(2)}) collective-permute-start(bf16[4,1024]{1,0:T(4,128)(2,1)S(1)} %slice.173), channel_id=1, source_target_pairs={{0,8},{1,9},{2,10},{3,11},{4,12},{5,13},{6,14},{7,15},{8,0},{9,1},... | collective-permute-start | bytes 24584 | tf_op jit(solution)/shard_map/ppermute | solution.py:41
where the time goes:
time: 144 us; the launch traced here: 142 us
  starting transfers between devices  60.6 us (42%)
  waiting for transfers between devices  50.5 us (35%)
  Pallas kernels  11.3 us (8%)
  matrix products  6.96 us (5%)
  local copies, waits for them, and re-layouts  6.93 us (5%)
  other arithmetic  4.96 us (3%)
    ppermute x9, waiting for transfers between devices, along_x(): lax.ppermute(v, 'dom', dom_pairs(lambda x, z, c: dom_index((x + k) % XS,...  21.8 us
    ppermute x9, starting transfers between devices, across_z(): lax.ppermute(v, 'dom', dom_pairs(lambda x, z, c: dom_index(x, z ^ bit, c)))  16.7 us
    ppermute x9, waiting for transfers between devices, across_z(): lax.ppermute(v, 'dom', dom_pairs(lambda x, z, c: dom_index(x, z ^ bit, c)))  15.5 us
    ppermute x10, starting transfers between devices, along_y(): lax.ppermute(v, 'group', [(y, (y + k) % GROUPS) for y in range(GROUPS)])  13.6 us
    ppermute x9, starting transfers between devices, along_x(): lax.ppermute(v, 'dom', dom_pairs(lambda x, z, c: dom_index((x + k) % XS,...  13.3 us
    pallas_call x11, Pallas kernels, call(): return kernel(*args)  11.3 us
    ppermute x4, starting transfers between devices, chip_step(): return lax.ppermute(v, 'dom', pairs)  10.2 us
    ppermute x4, waiting for transfers between devices, chip_step(): return lax.ppermute(v, 'dom', pairs)  7.64 us
  transfers between devices with their start and end apart: 37, of which 16 were waited for; matrix products, arithmetic and copies ran while one was open for 5% of the time, Pallas kernels for 5%

commit v1 on v0

v1 whole, which is shorter than its diff:
```python
import jax
import jax.numpy as jnp
from jax import lax
from jax.experimental import pallas as pl
from jax.experimental.pallas import tpu as pltpu
from jax.sharding import PartitionSpec as P


BLK = 128
HUB_DEV = 4
CORES = 2
XS = 4
ZS = 8
GROUPS = 4
F32 = jnp.float32
BF16 = jnp.bfloat16


def dom_index(x, z, c):
    return (x * ZS + z) * CORES + c


def dom_pairs(target):
    pairs = []
    for x in range(XS):
        for z in range(ZS):
            for c in range(CORES):
                pairs.append((dom_index(x, z, c), target(x, z, c)))
    return pairs


def swap(v):
    return lax.ppermute(v, "dom", dom_pairs(lambda x, z, c: dom_index(x, z, 1 - c)))


def along_x(v, k):
    return lax.ppermute(v, "dom", dom_pairs(lambda x, z, c: dom_index((x + k) % XS, z, c)))


def along_z(v, k):
    return lax.ppermute(
        v, "dom", dom_pairs(lambda x, z, c: dom_index(x, (z + (k if c else -k)) % ZS, c))
    )


def along_y(v, k):
    return lax.ppermute(v, "group", [(y, (y + k) % GROUPS) for y in range(GROUPS)])


def chip_step(v, even_by):
    count = XS * ZS * CORES
    return lax.ppermute(
        v, "dom", [(d, (d + (even_by if d % 2 == 0 else -even_by)) % count) for d in range(count)]
    )


def first_step(v):
    return chip_step(v, -2)


def second_step(v):
    return chip_step(v, 2)


def offset_of(order):
    return (order // 2 + 1) * (1 - 2 * (order % 2))


def dot(a, b):
    return lax.dot_general(a, b, (((1,), (0,)), ((), ())), preferred_element_type=F32)


def dot_tn(a, b):
    return lax.dot_general(a, b, (((0,), (0,)), ((), ())), preferred_element_type=F32)


def dot_nt(a, b):
    return lax.dot_general(a, b, (((1,), (1,)), ((), ())), preferred_element_type=F32)


def relative_rows(shape, with_group, here, y):
    c = here & 1
    z = (here >> 1) & (ZS - 1)
    x = here >> 4
    r = lax.broadcasted_iota(jnp.int32, shape, 0)
    at = 4 if with_group else 2
    kz = ((r >> (at + 2)) & 1) + (((r >> (at + 1)) & 1) << 1) + (((r >> at) & 1) << 2)
    cc = c ^ (r >> (9 if with_group else 7))
    zz = (z - (2 * cc - 1) * kz) & (ZS - 1)
    low = r & 3
    if with_group:
        xx = (x + (r >> 2)) & 3
        yy = (y + (r >> 7)) & 3
        return (yy << 8) + (xx << 6) + (zz << 3) + (cc << 2) + low
    xx = (x + (r >> 5)) & 3
    return (xx << 6) + (zz << 3) + (cc << 2) + low


VM = pl.BlockSpec(memory_space=pltpu.VMEM)
SM = pl.BlockSpec(memory_space=pltpu.SMEM)
ANY = pl.BlockSpec(memory_space=pl.ANY)


def call(body, specs, outs, flops, *args):
    shapes = [jax.ShapeDtypeStruct(s, d) for s, d in outs]
    moved = sum(a.size * a.dtype.itemsize for a in args) + sum(s.size * s.dtype.itemsize for s in shapes)
    kernel = pl.pallas_call(
        body,
        out_shape=shapes,
        in_specs=specs,
        out_specs=[VM] * len(shapes),
        cost_estimate=pl.CostEstimate(flops=flops, bytes_accessed=moved, transcendentals=0),
        compiler_params=pltpu.CompilerParams(vmem_limit_bytes=16 * 1024 * 1024),
    )
    return kernel(*args)


def lane_loop(width, body):
    def step(i, carry):
        body(pl.multiple_of(i * 256, 256))
        return carry

    lax.fori_loop(0, width // 256, step, 0)


def hub_kernel(asked_ref, hub_ref, f_ref, rel_ref, pay_ref, f0_ref, mine_ref):
    target = relative_rows((256, 256), False, lax.axis_index("dom"), 0)
    col = lax.broadcasted_iota(jnp.int32, (256, 256), 1)
    perm = jnp.where(target == col, 1.0, 0.0).astype(BF16)
    ordered = dot(perm, hub_ref[...])
    rel = ordered.astype(BF16)
    rel_ref[...] = jnp.transpose(ordered).astype(BF16)

    def some(n):
        lanes = pl.ds(n, 256)
        for t in range(2):
            p = dot(rel, f_ref[t, :, lanes])
            mine_ref[:, pl.ds(t * 1024 + n, 256)] = p[:128]
            pay_ref[t * 128 : t * 128 + 128, lanes] = p[128:].astype(BF16)
        pay_ref[256:512, lanes] = f_ref[0, :, lanes]
        f0_ref[:, lanes] = f_ref[0, :, lanes]

    lane_loop(1024, some)


def perm_kernel(out_ref):
    target = relative_rows((1024, 128), True, lax.axis_index("dom"), lax.axis_index("group"))
    col = lax.broadcasted_iota(jnp.int32, (1024, 128), 1)
    off = target - col
    for n in range(8):
        out_ref[:, n * 128 : n * 128 + 128] = jnp.where(off == n * 128, 1.0, 0.0).astype(BF16)


def table_kernel(present, asked_ref, b_ref, a_ref, roles_ref, roles_t_ref, local_ref, local_t_ref):
    here = lax.axis_index("dom")
    c = here & 1
    asked = asked_ref[0, here]
    for r in range(4):
        for b in range(2):
            total = None
            for o in (r, r ^ 1):
                source = here + offset_of(o)
                inside = ((r ^ c) == o) & (source >= 0) & (source < XS * ZS * CORES)
                for j in range(2):
                    s = 2 * o + j
                    gate = jnp.where(inside & (asked[o : o + 1, j : j + 1] == b), 1.0, 0.0)
                    term = b_ref[:, s * BLK : s * BLK + BLK].astype(F32) * gate
                    total = term if total is None else total + term
            at = (2 * r + b) * BLK
            roles_ref[:, at : at + BLK] = total.astype(BF16)
            roles_t_ref[at : at + BLK, :] = jnp.transpose(total).astype(BF16)
    for i in range(2):
        for j in range(2):
            gate = present[i, j].astype(F32)
            tile = a_ref[i * BLK : i * BLK + BLK, j * BLK : j * BLK + BLK].astype(F32) * gate
            local_ref[i * BLK : i * BLK + BLK, j * BLK : j * BLK + BLK] = tile.astype(BF16)
            local_t_ref[j * BLK : j * BLK + BLK, i * BLK : i * BLK + BLK] = jnp.transpose(tile).astype(BF16)


def open_kernel(got_ref, mine_ref, keep_ref, *send_refs):
    def some(n):
        for t in range(2):
            lanes = pl.ds(t * 1024 + n, 256)
            part = mine_ref[:, lanes] + got_ref[t * 128 : t * 128 + 128, pl.ds(n, 256)].astype(F32)
            keep_ref[:, lanes] = part[:32]
            for k in range(3):
                send_refs[k][:, lanes] = part[32 * k + 32 : 32 * k + 64].astype(BF16)

    lane_loop(1024, some)


def total_kernel(after, roles, local, f_ref, pair_ref, far_ref, first_ref, out_ref):
    def some(n):
        lanes = pl.ds(n, 256)
        bound = (
            dot(roles[:, :256], pair_ref[256:512, lanes])
            + dot(roles[:, 256:512], far_ref[:, lanes])
            + dot(roles[:, 512:768], first_ref[:, lanes])
        )
        for t in range(2):
            out_ref[t * 256 : t * 256 + 256, lanes] = bound + dot(local[...], f_ref[t, :, lanes])

    lane_loop(1024, some)


def agg_kernel(offs, roles, second_ref, total_ref, own_ref, g1_ref, g2_ref, g3_ref, agg_ref):
    ids = lax.broadcasted_iota(jnp.int32, (64, 256), 0)

    def some(n):
        lanes = pl.ds(n, 256)
        bound = dot(roles[:, 768:], second_ref[:, lanes])
        for t in range(2):
            at_t = pl.ds(t * 1024 + n, 256)
            hubs = own_ref[:, at_t] + (
                g1_ref[:, at_t].astype(F32) + g2_ref[:, at_t].astype(F32) + g3_ref[:, at_t].astype(F32)
            )
            for i in range(HUB_DEV):
                at = t * 256 + i * 64
                extra = jnp.where(ids == offs[0, i], hubs[i : i + 1], 0.0)
                rest = total_ref[at : at + 64, lanes] + bound[i * 64 : i * 64 + 64]
                agg_ref[at : at + 64, lanes] = (rest + extra).astype(BF16)

    lane_loop(1024, some)


def send_kernel(offs, roles_t, dagg_ref, mirror_ref, *first_refs):
    cols = lax.broadcasted_iota(jnp.int32, (8, 256), 1)
    rows = lax.broadcasted_iota(jnp.int32, (8, 256), 0)
    where = jnp.where(
        rows == 0, offs[0, 0], jnp.where(rows == 1, offs[0, 1], jnp.where(rows == 2, offs[0, 2], offs[0, 3]))
    )
    pick = jnp.where((cols == rows * 64 + where) & (rows < HUB_DEV), 1.0, 0.0).astype(BF16)

    def some(n):
        lanes = pl.ds(n, 256)
        for t in range(2):
            d = dagg_ref[t * 256 : t * 256 + 256, lanes]
            mirror_ref[:, pl.ds(t * 1024 + n, 256)] = dot(pick, d)[:HUB_DEV].astype(BF16)
            first_refs[t][:, lanes] = dot(roles_t[768:, :], d).astype(BF16)

    lane_loop(1024, some)


def role_kernel(r, roles_t, dagg_ref, out_ref):
    def some(n):
        lanes = pl.ds(n, 256)
        for t in range(2):
            rows = slice(t * 256, t * 256 + 256)
            out_ref[rows, lanes] = dot(roles_t[r * 256 : r * 256 + 256, :], dagg_ref[rows, lanes]).astype(BF16)

    lane_loop(1024, some)


def near_kernel(*refs):
    role_kernel(0, *refs)


def far_kernel(*refs):
    role_kernel(1, *refs)


def through_kernel(roles_t, dagg_ref, got_ref, out_ref):
    def some(n):
        lanes = pl.ds(n, 256)
        for t in range(2):
            rows = slice(t * 256, t * 256 + 256)
            mine = dot(roles_t[512:768, :], dagg_ref[rows, lanes])
            out_ref[rows, lanes] = (mine + got_ref[rows, lanes].astype(F32)).astype(BF16)

    lane_loop(1024, some)


def base_kernel(local_t, dagg_ref, pair_ref, first0_ref, first1_ref, second_ref, base_ref, carried_ref):
    def some(n):
        lanes = pl.ds(n, 256)
        firsts = (first0_ref, first1_ref)
        local = [dot(local_t[...], dagg_ref[t * 256 : t * 256 + 256, lanes]) for t in range(2)]
        back = [
            pair_ref[t * 256 : t * 256 + 256, lanes].astype(F32)
            + firsts[t][:, lanes].astype(F32)
            + second_ref[t * 256 : t * 256 + 256, lanes].astype(F32)
            for t in range(2)
        ]
        base_ref[:256, lanes] = local[0]
        base_ref[256:, lanes] = local[1] + back[0]
        carried_ref[:, lanes] = back[1].astype(BF16)

    lane_loop(1024, some)


def grad_kernel(base_ref, rel_t, own_ref, got_ref, out_ref):
    def some(n):
        for t in range(2):
            lanes = pl.ds(t * 1024 + n, 256)
            hub = dot(rel_t[:, :128], own_ref[:, lanes]) + dot(rel_t[:, 128:], got_ref[:, lanes])
            out_ref[t, :, pl.ds(n, 256)] = (base_ref[t * 256 : t * 256 + 256, pl.ds(n, 256)] + hub).astype(BF16)

    lane_loop(1024, some)


def join_kernel(own_ref, one_ref, two_ref, three_ref, out_ref):
    out_ref[:32, :] = own_ref[...]
    out_ref[32:64, :] = one_ref[...]
    out_ref[64:96, :] = two_ref[...]
    out_ref[96:, :] = three_ref[...]


def per_device(
    features,
    adjacency,
    tile_mask,
    boundary_adj,
    boundary_blocks,
    hub_adj,
    hub_offsets,
    weight,
    cotangent,
):
    steps, nodes, width = features.shape
    both = steps * nodes
    mm = 2 * nodes * nodes * width

    rel_t, payload, first, mine = call(
        hub_kernel,
        [VM, VM, VM],
        [((256, 256), BF16), ((512, width), BF16), ((nodes, width), BF16), ((128, 2 * width), F32)],
        2 * mm,
        boundary_blocks,
        hub_adj,
        features,
    )
    from_pair = swap(payload)
    from_first = first_step(first)
    from_second = second_step(first)

    roles, roles_t, local, local_t = call(
        table_kernel,
        [SM, VM, VM, VM],
        [((nodes, width), BF16), ((width, nodes), BF16), ((nodes, nodes), BF16), ((nodes, nodes), BF16)],
        mm,
        tile_mask,
        boundary_blocks,
        boundary_adj,
        adjacency,
    )

    (perm,) = call(perm_kernel, [], [((width, width), BF16)], mm)
    part, *sends = call(
        open_kernel,
        [VM, VM],
        [((32, 2 * width), F32)] + [((32, 2 * width), BF16)] * 3,
        mm,
        from_pair,
        mine,
    )
    gots = [along_x(sends[k - 1], k) for k in (1, 3, 2)]
    from_far = swap(from_first)
    part = part + (gots[0].astype(F32) + gots[1].astype(F32) + gots[2].astype(F32))
    marks = []
    for k, rows in ((1, 16), (2, 8), (4, 4)):
        sent = part[rows:].astype(BF16)
        marks.append(sent)
        got = along_z(sent, -k)
        part = part[:rows] + got.astype(F32)
    sent = part.astype(BF16)
    gots = [along_y(sent, k) for k in (1, 3, 2)]

    (total,) = call(
        total_kernel,
        [ANY, VM, VM, VM, VM, VM, VM],
        [((both, width), F32)],
        6 * mm,
        marks[1],
        roles,
        local,
        features,
        from_pair,
        from_far,
        from_first,
    )
    (agg,) = call(
        agg_kernel,
        [SM, VM, VM, VM, VM, VM, VM, VM],
        [((both, width), BF16)],
        mm,
        hub_offsets,
        roles,
        from_second,
        total,
        part,
        *gots,
    )
    pre = dot_nt(agg, weight)
    sig = jax.nn.sigmoid(pre)
    act = (pre * sig).astype(BF16)
    gpre = (cotangent.reshape(both, width).astype(F32) * sig * (1.0 + pre * (1.0 - sig))).astype(BF16)

    gpre_rel = lax.optimization_barrier(dot_nt(gpre, perm).astype(BF16))
    got_w = swap(dot_tn(gpre_rel[:, 512:], agg).astype(BF16))
    dagg = dot(gpre, weight).astype(BF16)

    (to_far,) = call(far_kernel, [VM, VM], [((both, width), BF16)], 2 * mm, roles_t, dagg)
    got_far = swap(to_far)
    mirror, *to_first = call(
        send_kernel,
        [SM, VM, VM],
        [((HUB_DEV, 2 * width), BF16)] + [((nodes, width), BF16)] * 2,
        2 * mm,
        hub_offsets,
        roles_t,
        dagg,
    )
    gots = [along_y(mirror, k) for k in (1, 3, 2)]
    (to_second,) = call(
        through_kernel, [VM, VM, VM], [((both, width), BF16)], 2 * mm, roles_t, dagg, got_far
    )
    back_second = second_step(to_second)
    back_first = [first_step(to_first[t]) for t in range(2)]
    (to_near,) = call(near_kernel, [VM, VM], [((both, width), BF16)], 2 * mm, roles_t, dagg)
    back_pair = swap(to_near)
    gathered = (
        mirror.astype(F32) + (gots[0].astype(F32) + gots[1].astype(F32) + gots[2].astype(F32))
    ).astype(BF16)

    wg = lax.optimization_barrier(dot_tn(gpre_rel[:, :512], agg)) + got_w.astype(F32)
    up = along_y(wg[256:320].astype(BF16), 1)
    down = along_y(wg[320:384].astype(BF16), 3)
    to_up = jnp.concatenate([wg[128:192] + up.astype(F32), wg[192:256]], axis=0).astype(BF16)
    to_down = jnp.concatenate([wg[384:448], wg[448:512] + down.astype(F32)], axis=0).astype(BF16)
    wg = wg[:128] + along_y(to_up, 1).astype(F32) + along_y(to_down, 3).astype(F32)
    for k, rows in ((1, 64), (2, 32), (4, 16)):
        got = along_z(wg[rows:].astype(BF16), -k)
        wg = wg[:rows] + got.astype(F32)
    sent = wg.astype(BF16)
    gots = [along_x(sent[4 * k : 4 * k + 4], k) for k in (1, 3, 2)]
    wg = wg[:4] + (gots[0].astype(F32) + gots[1].astype(F32) + gots[2].astype(F32))

    for k in (4, 2, 1):
        gathered = jnp.concatenate([gathered, along_z(gathered, k)], axis=0)
        gathered = lax.optimization_barrier(gathered)
    gots = [along_x(gathered, -k) for k in (1, 3, 2)]
    (joined,) = call(
        join_kernel, [VM] * 4, [((128, 2 * width), BF16)], mm, gathered, gots[0], gots[2], gots[1]
    )
    other = swap(joined)

    base, carried = call(
        base_kernel,
        [VM] * 6,
        [((both, width), F32), ((nodes, width), BF16)],
        2 * mm,
        local_t,
        dagg,
        back_pair,
        *back_first,
        back_second,
    )
    (grads,) = call(
        grad_kernel, [VM] * 4, [((steps, nodes, width), BF16)], 2 * mm, base, rel_t, joined, other
    )
    scale = (both * GROUPS * XS * ZS * CORES) ** (-0.5)
    return act.reshape(steps, nodes, width), grads, carried, wg * scale


def solution(mesh):
    return jax.shard_map(
        per_device,
        mesh=mesh,
        in_specs=(
            P(None, ("group", "dom"), None),
            P(("group", "dom"), None),
            P(("group", "dom"), None),
            P(("group", "dom"), None),
            P("group", None, None, None),
            P(None, ("group", "dom")),
            P("group", "dom"),
            P(),
            P(None, ("group", "dom"), None),
        ),
        out_specs=(
            P(None, ("group", "dom"), None),
            P(None, ("group", "dom"), None),
            P(("group", "dom"), None),
            P(("group", "dom"), None),
        ),
        check_vma=False,
    )
```

time: 144 us -> 146 us (1.014); the launches traced: 142 us -> 146 us
  starting transfers between devices: 60.6 us -> 73.2 us
  waiting for transfers between devices: 50.5 us -> 45.2 us
  Pallas kernels: 11.3 us -> 15.1 us
  local copies, waits for them, and re-layouts: 6.93 us -> 3.23 us
  other arithmetic: 4.96 us -> 1.49 us
    ppermute x5 -> x6, starting transfers between devices: 6.76 us -> 20.5 us  [swap(): lax.ppermute(v, 'dom', dom_pairs(lambda x, z, c: dom_index(x, z, 1 - c)))]
    ppermute x13 -> x14, waiting for transfers between devices: 23.1 us -> 15.3 us  [the longest x5 8.36 us: chip_step(): lax.ppermute(v, 'dom', [(d, (d + (even_by if d % 2 == 0 else -even_by)) %...]
    ppermute x9, starting transfers between devices: 13.3 us -> 9.21 us  [along_x(): lax.ppermute(v, 'dom', dom_pairs(lambda x, z, c: dom_index((x + k) % XS,...]
    pallas_call x11 -> x13, Pallas kernels: 11.3 us -> 15.1 us  [call(): return kernel(*args)]
    ppermute x13 -> x14, starting transfers between devices: 26.9 us -> 30.6 us  [the longest x9 24 us: along_z(): lax.ppermute(v, 'dom', dom_pairs(lambda x, z, c: dom_index(x, (z + (k if...]
    unnamed x26 -> x19, local copies, waits for them, and re-layouts: 4.99 us -> 3.12 us
    convert_element_type x1, other arithmetic: 1.76 us -> 0.01 us  [per_device(): sent = wg.astype(BF16)]
    ppermute x5 -> x6, waiting for transfers between devices: 2.3 us -> 3.84 us  [swap(): lax.ppermute(v, 'dom', dom_pairs(lambda x, z, c: dom_index(x, z, 1 - c)))]
  transfers between devices with their start and end apart: 37 -> 39, of which waited for: 16 -> 17; matrix products, arithmetic and copies ran while one was open for 5% -> 2% of each run, Pallas kernels for 5% -> 7%
where the time goes in v1:
time: 146 us
  starting transfers between devices  73.2 us (50%)
  waiting for transfers between devices  45.2 us (31%)
  Pallas kernels  15.1 us (10%)
  matrix products  7.05 us (5%)
  local copies, waits for them, and re-layouts  3.23 us (2%)
  other arithmetic  1.49 us (1%)
    ppermute x9, starting transfers between devices, along_z(): lax.ppermute(v, 'dom', dom_pairs(lambda x, z, c: dom_index(x, (z + (k if...  24 us
    ppermute x9, waiting for transfers between devices, along_x(): lax.ppermute(v, 'dom', dom_pairs(lambda x, z, c: dom_index((x + k) % XS,...  22.7 us
    ppermute x6, starting transfers between devices, swap(): lax.ppermute(v, 'dom', dom_pairs(lambda x, z, c: dom_index(x, z, 1 - c)))  20.5 us
    pallas_call x13, Pallas kernels, call(): return kernel(*args)  15.1 us
    ppermute x10, starting transfers between devices, along_y(): lax.ppermute(v, 'group', [(y, (y + k) % GROUPS) for y in range(GROUPS)])  12.9 us
    ppermute x9, starting transfers between devices, along_x(): lax.ppermute(v, 'dom', dom_pairs(lambda x, z, c: dom_index((x + k) % XS,...  9.21 us
    ppermute x5, waiting for transfers between devices, chip_step(): lax.ppermute(v, 'dom', [(d, (d + (even_by if d % 2 == 0 else -even_by)) %...  8.36 us
    ppermute x9, waiting for transfers between devices, along_z(): lax.ppermute(v, 'dom', dom_pairs(lambda x, z, c: dom_index(x, (z + (k if...  6.96 us
  transfers between devices with their start and end apart: 39, of which 17 were waited for; matrix products, arithmetic and copies ran while one was open for 2% of the time, Pallas kernels for 7%

profile of v1, /device:TPU:1, one launch (start us, length us, event | category | flops | bytes accessed | tf_op | source)
XLA Modules:
  0.0 146.3 jit_solution(1112230249426240577)
XLA Ops:
  0.6 1.0 copy.13.asked_ref
  1.6 1.2 copy-done.1
  2.8 0.9 copy-done.4
  3.7 1.3 shard_map.121
  5.1 3.3 %collective-permute-start.1 = (bf16[512,1024]{1,0:T(8,128)(2,1)S(1)}, bf16[512,1024]{1,0:T(8,128)(2,1)S(1)}, u32[]{:S(2)}, u32[]{:S(2)}) collective-permute-start(bf16[512,1024]{1,0:T(8,128)(2,1)S(1)} %get-tuple-element.23), channel_id=1, source_target_pairs={{0,1},{1,0},{2,3},{3,2},{4,5},{5,4},{6,7},{7,6},{8,9},{9,8},{10,11... | collective-permute-start | bytes 3145736 | tf_op jit(solution)/shard_map/ppermute | solution.py:33
  8.3 2.3 %collective-permute-done.1.got_ref.pair_ref = bf16[512,1024]{1,0:T(8,128)(2,1)S(1)} collective-permute-done((bf16[512,1024]{1,0:T(8,128)(2,1)S(1)}, bf16[512,1024]{1,0:T(8,128)(2,1)S(1)}, u32[]{:S(2)}, u32[]{:S(2)}) %collective-permute-start.1) | collective-permute-done | bytes 1048608 | tf_op jit(solution)/shard_map/ppermute | solution.py:33
  10.9 2.7 %collective-permute-start.3 = (bf16[32,2048]{1,0:T(8,128)(2,1)S(1)}, bf16[32,2048]{1,0:T(8,128)(2,1)S(1)}, u32[]{:S(2)}, u32[]{:S(2)}) collective-permute-start(bf16[32,2048]{1,0:T(8,128)(2,1)S(1)} %get-tuple-element.27), channel_id=1, source_target_pairs={{0,48},{1,49},{2,50},{3,51},{4,52},{5,53},{6,54},{7,55},{8,56},{9,... | collective-permute-start | bytes 393224 | tf_op jit(solution)/shard_map/ppermute | solution.py:37
  13.6 3.2 %collective-permute-done.2 = bf16[32,2048]{1,0:T(8,128)(2,1)S(1)} collective-permute-done((bf16[32,2048]{1,0:T(8,128)(2,1)S(1)}, bf16[32,2048]{1,0:T(8,128)(2,1)S(1)}, u32[]{:S(2)}, u32[]{:S(2)}) %collective-permute-start.2) | collective-permute-done | bytes 131104 | tf_op jit(solution)/shard_map/ppermute | solution.py:37
  16.8 1.9 %collective-permute-done.3 = bf16[32,2048]{1,0:T(8,128)(2,1)S(1)} collective-permute-done((bf16[32,2048]{1,0:T(8,128)(2,1)S(1)}, bf16[32,2048]{1,0:T(8,128)(2,1)S(1)}, u32[]{:S(2)}, u32[]{:S(2)}) %collective-permute-start.3) | collective-permute-done | bytes 131104 | tf_op jit(solution)/shard_map/ppermute | solution.py:37
  18.7 0.5 collective-permute-done.4
  19.3 5.3 %collective-permute-start.5 = (bf16[16,2048]{1,0:T(8,128)(2,1)S(1)}, bf16[16,2048]{1,0:T(8,128)(2,1)S(1)}, u32[]{:S(2)}, u32[]{:S(2)}) collective-permute-start(bf16[16,2048]{1,0:T(8,128)(2,1)S(1)} %slice.165), channel_id=1, source_target_pairs={{0,2},{1,15},{2,4},{3,1},{4,6},{5,3},{6,8},{7,5},{8,10},{9,7},{10,... | collective-permute-start | bytes 196616 | tf_op jit(solution)/shard_map/ppermute | solution.py:41
  24.6 1.3 collective-permute-done.5
  26.0 2.3 %collective-permute-start.8 = (bf16[8,2048]{1,0:T(8,128)(2,1)S(1)}, bf16[8,2048]{1,0:T(8,128)(2,1)S(1)}, u32[]{:S(2)}, u32[]{:S(2)}) collective-permute-start(bf16[8,2048]{1,0:T(8,128)(2,1)S(1)} %slice.167.after), channel_id=1, source_target_pairs={{0,4},{1,13},{2,6},{3,15},{4,8},{5,1},{6,10},{7,3},{8,12},{9,5},{1... | collective-permute-start | bytes 98312 | tf_op jit(solution)/shard_map/ppermute | solution.py:41
  28.3 1.8 %collective-permute-start = (bf16[256,1024]{1,0:T(8,128)(2,1)S(1)}, bf16[256,1024]{1,0:T(8,128)(2,1)S(1)}, u32[]{:S(2)}, u32[]{:S(2)}) collective-permute-start(bf16[256,1024]{1,0:T(8,128)(2,1)S(1)} %get-tuple-element.22), channel_id=1, source_target_pairs={{0,2},{1,63},{2,4},{3,1},{4,6},{5,3},{6,8},{7,5},{8,10},{9,7},{10,... | collective-permute-start | bytes 1572872 | tf_op jit(solution)/shard_map/ppermute | solution.py:52
  30.1 8.3 %collective-permute-done.6.first_ref = bf16[256,1024]{1,0:T(8,128)(2,1)S(1)} collective-permute-done((bf16[256,1024]{1,0:T(8,128)(2,1)S(1)}, bf16[256,1024]{1,0:T(8,128)(2,1)S(1)}, u32[]{:S(2)}, u32[]{:S(2)}) %collective-permute-start.6) | collective-permute-done | bytes 524320 | tf_op jit(solution)/shard_map/ppermute | solution.py:52
  38.5 0.3 collective-permute-start.7
  38.8 4.3 %collective-permute-start.9 = (bf16[4,2048]{1,0:T(4,128)(2,1)S(1)}, bf16[4,2048]{1,0:T(4,128)(2,1)S(1)}, u32[]{:S(2)}, u32[]{:S(2)}) collective-permute-start(bf16[4,2048]{1,0:T(4,128)(2,1)S(1)} %slice.168), channel_id=1, source_target_pairs={{0,8},{1,9},{2,10},{3,11},{4,12},{5,13},{6,14},{7,15},{8,0},{9,1},... | collective-permute-start | bytes 49160 | tf_op jit(solution)/shard_map/ppermute | solution.py:41
  43.1 1.1 shard_map.132
  44.3 1.2 shard_map.120
  45.5 1.4 collective-permute-start.10
  46.9 1.5 %collective-permute-start.11 = (bf16[4,2048]{1,0:T(4,128)(2,1)S(1)}, bf16[4,2048]{1,0:T(4,128)(2,1)S(1)}, u32[]{:S(2)}, u32[]{:S(2)}) collective-permute-start(bf16[4,2048]{1,0:T(4,128)(2,1)S(1)} %get-tuple-element.42), channel_id=1, source_target_pairs={{0,192},{64,0},{128,64},{192,128},{1,193},{65,1},{129,65},{193,129... | collective-permute-start | bytes 49160 | tf_op jit(solution)/shard_map/ppermute | solution.py:47
  48.4 1.6 %collective-permute-start.12 = (bf16[4,2048]{1,0:T(4,128)(2,1)S(1)}, bf16[4,2048]{1,0:T(4,128)(2,1)S(1)}, u32[]{:S(2)}, u32[]{:S(2)}) collective-permute-start(bf16[4,2048]{1,0:T(4,128)(2,1)S(1)} %get-tuple-element.42), channel_id=1, source_target_pairs={{0,128},{64,192},{128,0},{192,64},{1,129},{65,193},{129,1},{193,65... | collective-permute-start | bytes 49160 | tf_op jit(solution)/shard_map/ppermute | solution.py:47
  50.0 1.4 shard_map.123.total_ref
  51.4 1.1 collective-permute-done.12.g3_ref
  52.6 1.4 shard_map.124
  54.0 3.0 %fusion.1 = (bf16[512,1024]{1,0:T(8,128)(2,1)S(1)}, bf16[512,1024]{1,0:T(8,128)(2,1)}) fusion(bf16[2,256,1024]{2,1,0:T(8,128)(2,1)S(1)} %copy-done.8, bf16[512,1024]{1,0:T(8,128)(2,1)S(1)} %shard_map.124, bf16[1024,1024]{1,0:T(8,128)(2,1)S(1)} %copy-done), kind=kOutput, calls=%fused_computation.2 | convolution fusion | flops 1080033280 | bytes 6291456 | tf_op jit(solution)/shard_map/dot_general | solution.py:78
  57.0 1.3 convolution_convert_fusion
  58.3 0.8 convolution_convert_fusion.2
  59.1 2.9 %collective-permute-start.28 = (bf16[512,1024]{1,0:T(8,128)(2,1)S(1)}, bf16[512,1024]{1,0:T(8,128)(2,1)S(1)}, u32[]{:S(2)}, u32[]{:S(2)}) collective-permute-start(bf16[512,1024]{1,0:T(8,128)(2,1)S(1)} %convolution_convert_fusion.2), channel_id=1, source_target_pairs={{0,1},{1,0},{2,3},{3,2},{4,5},{5,4},{6,7},{7,6},{8,9},{9,8},{10,11... | collective-permute-start | bytes 3145736 | tf_op jit(solution)/shard_map/ppermute | solution.py:33
  62.0 0.7 fusion.4
  62.7 1.5 %collective-permute-done.28 = bf16[512,1024]{1,0:T(8,128)(2,1)S(1)} collective-permute-done((bf16[512,1024]{1,0:T(8,128)(2,1)S(1)}, bf16[512,1024]{1,0:T(8,128)(2,1)S(1)}, u32[]{:S(2)}, u32[]{:S(2)}) %collective-permute-start.28) | collective-permute-done | bytes 1048608 | tf_op jit(solution)/shard_map/ppermute | solution.py:33
  64.2 0.5 fusion.10
  64.9 2.6 %collective-permute-start.31 = (bf16[64,1024]{1,0:T(8,128)(2,1)S(1)}, bf16[64,1024]{1,0:T(8,128)(2,1)S(1)}, u32[]{:S(2)}, u32[]{:S(2)}) collective-permute-start(bf16[64,1024]{1,0:T(8,128)(2,1)S(1)} %get-tuple-element.49), channel_id=1, source_target_pairs={{0,192},{64,0},{128,64},{192,128},{1,193},{65,1},{129,65},{193,129... | collective-permute-start | bytes 393224 | tf_op jit(solution)/shard_map/ppermute | solution.py:47
  67.5 1.3 convolution_convert_fusion.1.refs_1_.dagg_ref
  68.8 1.6 %shard_map.126 = (bf16[4,2048]{1,0:T(4,128)(2,1)S(1)}, bf16[256,1024]{1,0:T(8,128)(2,1)S(1)}, bf16[256,1024]{1,0:T(8,128)(2,1)S(1)}) custom-call(s32[1,4]{1,0:T(1,128)S(1)} %copy-done.6, bf16[1024,256]{1,0:T(8,128)(2,1)S(1)} %get-tuple-element.31.refs_0_.roles_t, bf16[512,1024]{1,0:T(8,128)(2,1)S(1)} %convolution_convert_fusion.1.refs_1_.dagg_ref), custom_call_target="tpu_custom_call" | custom-call | flops 268435456 | bytes 2637840 | tf_op jit(solution)/shard_map/pallas_call | solution.py:115
  70.5 2.7 %collective-permute-start.19 = (bf16[4,2048]{1,0:T(4,128)(2,1)S(1)}, bf16[4,2048]{1,0:T(4,128)(2,1)S(1)}, u32[]{:S(2)}, u32[]{:S(2)}) collective-permute-start(bf16[4,2048]{1,0:T(4,128)(2,1)S(1)} %get-tuple-element.36), channel_id=1, source_target_pairs={{0,192},{64,0},{128,64},{192,128},{1,193},{65,1},{129,65},{193,129... | collective-permute-start | bytes 49160 | tf_op jit(solution)/shard_map/ppermute | solution.py:47
  73.2 0.9 shard_map.127
  74.1 0.9 shard_map.125
  75.1 1.6 %collective-permute-start.16 = (bf16[512,1024]{1,0:T(8,128)(2,1)S(1)}, bf16[512,1024]{1,0:T(8,128)(2,1)S(1)}, u32[]{:S(2)}, u32[]{:S(2)}) collective-permute-start(bf16[512,1024]{1,0:T(8,128)(2,1)S(1)} %shard_map.127), channel_id=1, source_target_pairs={{0,1},{1,0},{2,3},{3,2},{4,5},{5,4},{6,7},{7,6},{8,9},{9,8},{10,11... | collective-permute-start | bytes 3145736 | tf_op jit(solution)/shard_map/ppermute | solution.py:33
  76.9 0.9 collective-permute-start.30
  77.8 2.1 %collective-permute-start.32 = (bf16[128,1024]{1,0:T(8,128)(2,1)S(1)}, bf16[128,1024]{1,0:T(8,128)(2,1)S(1)}, u32[]{:S(2)}, u32[]{:S(2)}) collective-permute-start(bf16[128,1024]{1,0:T(8,128)(2,1)S(1)} %pad_maximum_fusion.1), channel_id=1, source_target_pairs={{0,192},{64,0},{128,64},{192,128},{1,193},{65,1},{129,65},{193,129... | collective-permute-start | bytes 786440 | tf_op jit(solution)/shard_map/ppermute | solution.py:47
  79.9 4.1 %collective-permute-start.21 = (bf16[4,2048]{1,0:T(4,128)(2,1)S(1)}, bf16[4,2048]{1,0:T(4,128)(2,1)S(1)}, u32[]{:S(2)}, u32[]{:S(2)}) collective-permute-start(bf16[4,2048]{1,0:T(4,128)(2,1)S(1)} %add_convert_fusion), channel_id=1, source_target_pairs={{0,8},{1,9},{2,10},{3,11},{4,12},{5,13},{6,14},{7,15},{8,0},{9,1},... | collective-permute-start | bytes 49160 | tf_op jit(solution)/shard_map/ppermute | solution.py:41
  84.0 1.9 %collective-permute-done.30 = bf16[128,1024]{1,0:T(8,128)(2,1)S(1)} collective-permute-done((bf16[128,1024]{1,0:T(8,128)(2,1)S(1)}, bf16[128,1024]{1,0:T(8,128)(2,1)S(1)}, u32[]{:S(2)}, u32[]{:S(2)}) %collective-permute-start.30) | collective-permute-done | bytes 262176 | tf_op jit(solution)/shard_map/ppermute | solution.py:47
  86.3 2.5 %collective-permute-start.33 = (bf16[64,1024]{1,0:T(8,128)(2,1)S(1)}, bf16[64,1024]{1,0:T(8,128)(2,1)S(1)}, u32[]{:S(2)}, u32[]{:S(2)}) collective-permute-start(bf16[64,1024]{1,0:T(8,128)(2,1)S(1)} %slice.163), channel_id=1, source_target_pairs={{0,2},{1,15},{2,4},{3,1},{4,6},{5,3},{6,8},{7,5},{8,10},{9,7},{10,... | collective-permute-start | bytes 393224 | tf_op jit(solution)/shard_map/ppermute | solution.py:41
  88.9 1.8 %collective-permute-done.33 = bf16[64,1024]{1,0:T(8,128)(2,1)S(1)} collective-permute-done((bf16[64,1024]{1,0:T(8,128)(2,1)S(1)}, bf16[64,1024]{1,0:T(8,128)(2,1)S(1)}, u32[]{:S(2)}, u32[]{:S(2)}) %collective-permute-start.33) | collective-permute-done | bytes 131104 | tf_op jit(solution)/shard_map/ppermute | solution.py:41
  90.8 2.0 %collective-permute-start.34 = (bf16[32,1024]{1,0:T(8,128)(2,1)S(1)}, bf16[32,1024]{1,0:T(8,128)(2,1)S(1)}, u32[]{:S(2)}, u32[]{:S(2)}) collective-permute-start(bf16[32,1024]{1,0:T(8,128)(2,1)S(1)} %slice.164), channel_id=1, source_target_pairs={{0,4},{1,13},{2,6},{3,15},{4,8},{5,1},{6,10},{7,3},{8,12},{9,5},{1... | collective-permute-start | bytes 196616 | tf_op jit(solution)/shard_map/ppermute | solution.py:41
  92.7 1.4 collective-permute-done.22
  94.1 1.1 collective-permute-start.23
  95.2 1.0 shard_map.128
  96.2 4.5 %collective-permute-start.17 = (bf16[512,1024]{1,0:T(8,128)(2,1)S(1)}, bf16[512,1024]{1,0:T(8,128)(2,1)S(1)}, u32[]{:S(2)}, u32[]{:S(2)}) collective-permute-start(bf16[512,1024]{1,0:T(8,128)(2,1)S(1)} %shard_map.128), channel_id=1, source_target_pairs={{0,2},{1,63},{2,4},{3,1},{4,6},{5,3},{6,8},{7,5},{8,10},{9,7},{10,... | collective-permute-start | bytes 3145736 | tf_op jit(solution)/shard_map/ppermute | solution.py:52
  100.7 2.2 %collective-permute-start.35 = (bf16[16,1024]{1,0:T(8,128)(2,1)S(1)}, bf16[16,1024]{1,0:T(8,128)(2,1)S(1)}, u32[]{:S(2)}, u32[]{:S(2)}) collective-permute-start(bf16[16,1024]{1,0:T(8,128)(2,1)S(1)} %slice.166), channel_id=1, source_target_pairs={{0,8},{1,9},{2,10},{3,11},{4,12},{5,13},{6,14},{7,15},{8,0},{9,1},... | collective-permute-start | bytes 98312 | tf_op jit(solution)/shard_map/ppermute | solution.py:41
  102.9 1.3 collective-permute-start.24
  104.3 1.1 collective-permute-start.25
  105.4 2.4 %collective-permute-done.35 = bf16[16,1024]{1,0:T(8,128)(2,1)S(1)} collective-permute-done((bf16[16,1024]{1,0:T(8,128)(2,1)S(1)}, bf16[16,1024]{1,0:T(8,128)(2,1)S(1)}, u32[]{:S(2)}, u32[]{:S(2)}) %collective-permute-start.35) | collective-permute-done | bytes 32800 | tf_op jit(solution)/shard_map/ppermute | solution.py:41
  108.0 13.0 %collective-permute-done.25.two_ref = bf16[32,2048]{1,0:T(8,128)(2,1)S(1)} collective-permute-done((bf16[32,2048]{1,0:T(8,128)(2,1)S(1)}, bf16[32,2048]{1,0:T(8,128)(2,1)S(1)}, u32[]{:S(2)}, u32[]{:S(2)}) %collective-permute-start.25) | collective-permute-done | bytes 131104 | tf_op jit(solution)/shard_map/ppermute | solution.py:37
  121.1 0.3 collective-permute-start.15
  121.4 2.2 %collective-permute-start.37 = (bf16[4,1024]{1,0:T(4,128)(2,1)S(1)}, bf16[4,1024]{1,0:T(4,128)(2,1)S(1)}, u32[]{:S(2)}, u32[]{:S(2)}) collective-permute-start(bf16[4,1024]{1,0:T(4,128)(2,1)S(1)} %get-tuple-element.54), channel_id=1, source_target_pairs={{0,48},{1,49},{2,50},{3,51},{4,52},{5,53},{6,54},{7,55},{8,56},{9,... | collective-permute-start | bytes 24584 | tf_op jit(solution)/shard_map/ppermute | solution.py:37
  123.6 0.8 collective-permute-done.37
  124.4 1.7 %collective-permute-start.38 = (bf16[4,1024]{1,0:T(4,128)(2,1)S(1)}, bf16[4,1024]{1,0:T(4,128)(2,1)S(1)}, u32[]{:S(2)}, u32[]{:S(2)}) collective-permute-start(bf16[4,1024]{1,0:T(4,128)(2,1)S(1)} %get-tuple-element.53), channel_id=1, source_target_pairs={{0,32},{1,33},{2,34},{3,35},{4,36},{5,37},{6,38},{7,39},{8,40},{9,... | collective-permute-start | bytes 24584 | tf_op jit(solution)/shard_map/ppermute | solution.py:37
  126.2 3.1 %collective-permute-done.38 = bf16[4,1024]{1,0:T(4,128)(2,1)S(1)} collective-permute-done((bf16[4,1024]{1,0:T(4,128)(2,1)S(1)}, bf16[4,1024]{1,0:T(4,128)(2,1)S(1)}, u32[]{:S(2)}, u32[]{:S(2)}) %collective-permute-start.38) | collective-permute-done | bytes 8224 | tf_op jit(solution)/shard_map/ppermute | solution.py:37
  129.3 12.4 %collective-permute-start.27 = (bf16[128,2048]{1,0:T(8,128)(2,1)S(1)}, bf16[128,2048]{1,0:T(8,128)(2,1)S(1)}, u32[]{:S(2)}, u32[]{:S(2)}) collective-permute-start(bf16[128,2048]{1,0:T(8,128)(2,1)S(1)} %shard_map.130.own_ref), channel_id=1, source_target_pairs={{0,1},{1,0},{2,3},{3,2},{4,5},{5,4},{6,7},{7,6},{8,9},{9,8},{10,11... | collective-permute-start | bytes 1572872 | tf_op jit(solution)/shard_map/ppermute | solution.py:33
  141.7 0.6 fusion.8
  142.4 1.8 %shard_map.129 = (f32[512,1024]{1,0:T(8,128)S(1)}, bf16[256,1024]{1,0:T(8,128)(2,1)}) custom-call(bf16[256,256]{1,0:T(8,128)(2,1)S(1)} %get-tuple-element.30.local_t, bf16[512,1024]{1,0:T(8,128)(2,1)S(1)} %convolution_convert_fusion.1.refs_1_.dagg_ref, bf16[512,1024]{1,0:T(8,128)(2,1)S(1)} %collective-permute-done.13.pair_ref, ...), custom_call_target="tpu_custom_call" | custom-call | flops 268435456 | bytes 6946816 | tf_op jit(solution)/shard_map/pallas_call | solution.py:115
  144.2 2.1 %shard_map.131 = bf16[2,256,1024]{2,1,0:T(8,128)(2,1)} custom-call(f32[512,1024]{1,0:T(8,128)S(1)} %get-tuple-element.34.base_ref, bf16[256,256]{1,0:T(8,128)(2,1)S(1)} %get-tuple-element.35.rel_t, bf16[128,2048]{1,0:T(8,128)(2,1)S(1)} %shard_map.130.own_ref, bf16[128,2048]{1,0:T(8,128)(2,1)S(1)} %collective-permute-done.27.got_ref), custom_call_target="tpu_custom_call" | custom-call | flops 268435456 | bytes 4325376 | tf_op jit(solution)/shard_map/pallas_call | solution.py:115
  (76 shorter events, 1.9 us)
Async XLA Ops:
  0.6 53.4 %copy-start = (bf16[1024,1024]{1,0:T(8,128)(2,1)S(1)}, bf16[1024,1024]{1,0:T(8,128)(2,1)}, u32[]{:S(2)}) copy-start(bf16[1024,1024]{1,0:T(8,128)(2,1)} %param.16) | copy-start | bytes 6291460
  1.6 1.2 copy-start.1
  2.8 0.9 copy-start.4
  5.1 5.6 %collective-permute-start.1 = (bf16[512,1024]{1,0:T(8,128)(2,1)S(1)}, bf16[512,1024]{1,0:T(8,128)(2,1)S(1)}, u32[]{:S(2)}, u32[]{:S(2)}) collective-permute-start(bf16[512,1024]{1,0:T(8,128)(2,1)S(1)} %get-tuple-element.23), channel_id=1, source_target_pairs={{0,1},{1,0},{2,3},{3,2},{4,5},{5,4},{6,7},{7,6},{8,9},{9,8},{10,11... | collective-permute-start | bytes 3145736 | tf_op jit(solution)/shard_map/ppermute | solution.py:33
  10.8 33.5 %copy-start.3 = (bf16[256,1024]{1,0:T(8,128)(2,1)S(1)}, bf16[256,1024]{1,0:T(8,128)(2,1)}, u32[]{:S(2)}) copy-start(bf16[256,1024]{1,0:T(8,128)(2,1)} %b_ref.1) | copy-start | bytes 1572868
  10.8 33.5 %copy-start.5 = (bf16[256,256]{1,0:T(8,128)(2,1)S(1)}, bf16[256,256]{1,0:T(8,128)(2,1)}, u32[]{:S(2)}) copy-start(bf16[256,256]{1,0:T(8,128)(2,1)} %a_ref.1) | copy-start | bytes 393220
  10.8 33.5 %copy-start.7 = (s32[2,2]{1,0:T(2,128)S(1)}, s32[2,2]{1,0:T(2,128)}, u32[]{:S(2)}) copy-start(s32[2,2]{1,0:T(2,128)} %present.1) | copy-start | bytes 52
  10.8 6.0 %collective-permute-start.2 = (bf16[32,2048]{1,0:T(8,128)(2,1)S(1)}, bf16[32,2048]{1,0:T(8,128)(2,1)S(1)}, u32[]{:S(2)}, u32[]{:S(2)}) collective-permute-start(bf16[32,2048]{1,0:T(8,128)(2,1)S(1)} %get-tuple-element.26), channel_id=1, source_target_pairs={{0,16},{1,17},{2,18},{3,19},{4,20},{5,21},{6,22},{7,23},{8,24},{9,... | collective-permute-start | bytes 393224 | tf_op jit(solution)/shard_map/ppermute | solution.py:37
  10.9 7.8 %collective-permute-start.3 = (bf16[32,2048]{1,0:T(8,128)(2,1)S(1)}, bf16[32,2048]{1,0:T(8,128)(2,1)S(1)}, u32[]{:S(2)}, u32[]{:S(2)}) collective-permute-start(bf16[32,2048]{1,0:T(8,128)(2,1)S(1)} %get-tuple-element.27), channel_id=1, source_target_pairs={{0,48},{1,49},{2,50},{3,51},{4,52},{5,53},{6,54},{7,55},{8,56},{9,... | collective-permute-start | bytes 393224 | tf_op jit(solution)/shard_map/ppermute | solution.py:37
  13.6 5.6 %collective-permute-start.4 = (bf16[32,2048]{1,0:T(8,128)(2,1)S(1)}, bf16[32,2048]{1,0:T(8,128)(2,1)S(1)}, u32[]{:S(2)}, u32[]{:S(2)}) collective-permute-start(bf16[32,2048]{1,0:T(8,128)(2,1)S(1)} %get-tuple-element.28), channel_id=1, source_target_pairs={{0,32},{1,33},{2,34},{3,35},{4,36},{5,37},{6,38},{7,39},{8,40},{9,... | collective-permute-start | bytes 393224 | tf_op jit(solution)/shard_map/ppermute | solution.py:37
  19.2 30.8 %copy-start.2 = (bf16[2,256,1024]{2,1,0:T(8,128)(2,1)S(1)}, bf16[2,256,1024]{2,1,0:T(8,128)(2,1)}, u32[]{:S(2)}) copy-start(bf16[2,256,1024]{2,1,0:T(8,128)(2,1)} %f_ref.3) | copy-start | bytes 3145732
  19.3 6.7 %collective-permute-start.5 = (bf16[16,2048]{1,0:T(8,128)(2,1)S(1)}, bf16[16,2048]{1,0:T(8,128)(2,1)S(1)}, u32[]{:S(2)}, u32[]{:S(2)}) collective-permute-start(bf16[16,2048]{1,0:T(8,128)(2,1)S(1)} %slice.165), channel_id=1, source_target_pairs={{0,2},{1,15},{2,4},{3,1},{4,6},{5,3},{6,8},{7,5},{8,10},{9,7},{10,... | collective-permute-start | bytes 196616 | tf_op jit(solution)/shard_map/ppermute | solution.py:41
  24.6 13.9 %collective-permute-start.6 = (bf16[256,1024]{1,0:T(8,128)(2,1)S(1)}, bf16[256,1024]{1,0:T(8,128)(2,1)S(1)}, u32[]{:S(2)}, u32[]{:S(2)}) collective-permute-start(bf16[256,1024]{1,0:T(8,128)(2,1)S(1)} %get-tuple-element.22), channel_id=1, source_target_pairs={{0,62},{1,3},{2,0},{3,5},{4,2},{5,7},{6,4},{7,9},{8,6},{9,11},{10,... | collective-permute-start | bytes 1572872 | tf_op jit(solution)/shard_map/ppermute | solution.py:52
  26.0 12.8 %collective-permute-start.8 = (bf16[8,2048]{1,0:T(8,128)(2,1)S(1)}, bf16[8,2048]{1,0:T(8,128)(2,1)S(1)}, u32[]{:S(2)}, u32[]{:S(2)}) collective-permute-start(bf16[8,2048]{1,0:T(8,128)(2,1)S(1)} %slice.167.after), channel_id=1, source_target_pairs={{0,4},{1,13},{2,6},{3,15},{4,8},{5,1},{6,10},{7,3},{8,12},{9,5},{1... | collective-permute-start | bytes 98312 | tf_op jit(solution)/shard_map/ppermute | solution.py:41
  28.3 23.1 %collective-permute-start = (bf16[256,1024]{1,0:T(8,128)(2,1)S(1)}, bf16[256,1024]{1,0:T(8,128)(2,1)S(1)}, u32[]{:S(2)}, u32[]{:S(2)}) collective-permute-start(bf16[256,1024]{1,0:T(8,128)(2,1)S(1)} %get-tuple-element.22), channel_id=1, source_target_pairs={{0,2},{1,63},{2,4},{3,1},{4,6},{5,3},{6,8},{7,5},{8,10},{9,7},{10,... | collective-permute-start | bytes 1572872 | tf_op jit(solution)/shard_map/ppermute | solution.py:52
  38.5 11.5 %collective-permute-start.7 = (bf16[256,1024]{1,0:T(8,128)(2,1)S(1)}, bf16[256,1024]{1,0:T(8,128)(2,1)S(1)}, u32[]{:S(2)}, u32[]{:S(2)}) collective-permute-start(bf16[256,1024]{1,0:T(8,128)(2,1)S(1)} %collective-permute-done.6.first_ref), channel_id=1, source_target_pairs={{0,1},{1,0},{2,3},{3,2},{4,5},{5,4},{6,7},{7,6},{8,9},{9,8},{10,11... | collective-permute-start | bytes 1572872 | tf_op jit(solution)/shard_map/ppermute | solution.py:33
  38.8 6.7 %collective-permute-start.9 = (bf16[4,2048]{1,0:T(4,128)(2,1)S(1)}, bf16[4,2048]{1,0:T(4,128)(2,1)S(1)}, u32[]{:S(2)}, u32[]{:S(2)}) collective-permute-start(bf16[4,2048]{1,0:T(4,128)(2,1)S(1)} %slice.168), channel_id=1, source_target_pairs={{0,8},{1,9},{2,10},{3,11},{4,12},{5,13},{6,14},{7,15},{8,0},{9,1},... | collective-permute-start | bytes 49160 | tf_op jit(solution)/shard_map/ppermute | solution.py:41
  45.5 5.9 %collective-permute-start.10 = (bf16[4,2048]{1,0:T(4,128)(2,1)S(1)}, bf16[4,2048]{1,0:T(4,128)(2,1)S(1)}, u32[]{:S(2)}, u32[]{:S(2)}) collective-permute-start(bf16[4,2048]{1,0:T(4,128)(2,1)S(1)} %get-tuple-element.42), channel_id=1, source_target_pairs={{0,64},{64,128},{128,192},{192,0},{1,65},{65,129},{129,193},{193,1... | collective-permute-start | bytes 49160 | tf_op jit(solution)/shard_map/ppermute | solution.py:47
  46.9 4.5 %collective-permute-start.11 = (bf16[4,2048]{1,0:T(4,128)(2,1)S(1)}, bf16[4,2048]{1,0:T(4,128)(2,1)S(1)}, u32[]{:S(2)}, u32[]{:S(2)}) collective-permute-start(bf16[4,2048]{1,0:T(4,128)(2,1)S(1)} %get-tuple-element.42), channel_id=1, source_target_pairs={{0,192},{64,0},{128,64},{192,128},{1,193},{65,1},{129,65},{193,129... | collective-permute-start | bytes 49160 | tf_op jit(solution)/shard_map/ppermute | solution.py:47
  48.4 4.1 %collective-permute-start.12 = (bf16[4,2048]{1,0:T(4,128)(2,1)S(1)}, bf16[4,2048]{1,0:T(4,128)(2,1)S(1)}, u32[]{:S(2)}, u32[]{:S(2)}) collective-permute-start(bf16[4,2048]{1,0:T(4,128)(2,1)S(1)} %get-tuple-element.42), channel_id=1, source_target_pairs={{0,128},{64,192},{128,0},{192,64},{1,129},{65,193},{129,1},{193,65... | collective-permute-start | bytes 49160 | tf_op jit(solution)/shard_map/ppermute | solution.py:47
  50.0 2.6 %copy-start.6 = (s32[1,4]{1,0:T(1,128)S(1)}, s32[1,4]{1,0:T(1,128)}, u32[]{:S(2)}) copy-start(s32[1,4]{1,0:T(1,128)} %offs.3) | copy-start | bytes 52
  52.6 1.5 %copy-start.8 = (bf16[2,256,1024]{2,1,0:T(8,128)(2,1)S(1)}, bf16[2,256,1024]{2,1,0:T(8,128)(2,1)}, u32[]{:S(2)}) copy-start(bf16[2,256,1024]{2,1,0:T(8,128)(2,1)} %param.17) | copy-start | bytes 3145732
  59.1 5.2 %collective-permute-start.28 = (bf16[512,1024]{1,0:T(8,128)(2,1)S(1)}, bf16[512,1024]{1,0:T(8,128)(2,1)S(1)}, u32[]{:S(2)}, u32[]{:S(2)}) collective-permute-start(bf16[512,1024]{1,0:T(8,128)(2,1)S(1)} %convolution_convert_fusion.2), channel_id=1, source_target_pairs={{0,1},{1,0},{2,3},{3,2},{4,5},{5,4},{6,7},{7,6},{8,9},{9,8},{10,11... | collective-permute-start | bytes 3145736 | tf_op jit(solution)/shard_map/ppermute | solution.py:33
  64.8 10.3 %collective-permute-start.29 = (bf16[64,1024]{1,0:T(8,128)(2,1)S(1)}, bf16[64,1024]{1,0:T(8,128)(2,1)S(1)}, u32[]{:S(2)}, u32[]{:S(2)}) collective-permute-start(bf16[64,1024]{1,0:T(8,128)(2,1)S(1)} %get-tuple-element.48), channel_id=1, source_target_pairs={{0,64},{64,128},{128,192},{192,0},{1,65},{65,129},{129,193},{193,1... | collective-permute-start | bytes 393224 | tf_op jit(solution)/shard_map/ppermute | solution.py:47
  64.9 11.8 %collective-permute-start.31 = (bf16[64,1024]{1,0:T(8,128)(2,1)S(1)}, bf16[64,1024]{1,0:T(8,128)(2,1)S(1)}, u32[]{:S(2)}, u32[]{:S(2)}) collective-permute-start(bf16[64,1024]{1,0:T(8,128)(2,1)S(1)} %get-tuple-element.49), channel_id=1, source_target_pairs={{0,192},{64,0},{128,64},{192,128},{1,193},{65,1},{129,65},{193,129... | collective-permute-start | bytes 393224 | tf_op jit(solution)/shard_map/ppermute | solution.py:47
  70.4 6.5 %collective-permute-start.18 = (bf16[4,2048]{1,0:T(4,128)(2,1)S(1)}, bf16[4,2048]{1,0:T(4,128)(2,1)S(1)}, u32[]{:S(2)}, u32[]{:S(2)}) collective-permute-start(bf16[4,2048]{1,0:T(4,128)(2,1)S(1)} %get-tuple-element.36), channel_id=1, source_target_pairs={{0,64},{64,128},{128,192},{192,0},{1,65},{65,129},{129,193},{193,1... | collective-permute-start | bytes 49160 | tf_op jit(solution)/shard_map/ppermute | solution.py:47
  70.5 7.3 %collective-permute-start.19 = (bf16[4,2048]{1,0:T(4,128)(2,1)S(1)}, bf16[4,2048]{1,0:T(4,128)(2,1)S(1)}, u32[]{:S(2)}, u32[]{:S(2)}) collective-permute-start(bf16[4,2048]{1,0:T(4,128)(2,1)S(1)} %get-tuple-element.36), channel_id=1, source_target_pairs={{0,192},{64,0},{128,64},{192,128},{1,193},{65,1},{129,65},{193,129... | collective-permute-start | bytes 49160 | tf_op jit(solution)/shard_map/ppermute | solution.py:47
  73.2 6.7 %collective-permute-start.20 = (bf16[4,2048]{1,0:T(4,128)(2,1)S(1)}, bf16[4,2048]{1,0:T(4,128)(2,1)S(1)}, u32[]{:S(2)}, u32[]{:S(2)}) collective-permute-start(bf16[4,2048]{1,0:T(4,128)(2,1)S(1)} %get-tuple-element.36), channel_id=1, source_target_pairs={{0,128},{64,192},{128,0},{192,64},{1,129},{65,193},{129,1},{193,65... | collective-permute-start | bytes 49160 | tf_op jit(solution)/shard_map/ppermute | solution.py:47
  75.1 20.1 %collective-permute-start.16 = (bf16[512,1024]{1,0:T(8,128)(2,1)S(1)}, bf16[512,1024]{1,0:T(8,128)(2,1)S(1)}, u32[]{:S(2)}, u32[]{:S(2)}) collective-permute-start(bf16[512,1024]{1,0:T(8,128)(2,1)S(1)} %shard_map.127), channel_id=1, source_target_pairs={{0,1},{1,0},{2,3},{3,2},{4,5},{5,4},{6,7},{7,6},{8,9},{9,8},{10,11... | collective-permute-start | bytes 3145736 | tf_op jit(solution)/shard_map/ppermute | solution.py:33
  76.7 65.7 %collective-permute-start.13 = (bf16[512,1024]{1,0:T(8,128)(2,1)S(1)}, bf16[512,1024]{1,0:T(8,128)(2,1)S(1)}, u32[]{:S(2)}, u32[]{:S(2)}) collective-permute-start(bf16[512,1024]{1,0:T(8,128)(2,1)S(1)} %shard_map.125), channel_id=1, source_target_pairs={{0,1},{1,0},{2,3},{3,2},{4,5},{5,4},{6,7},{7,6},{8,9},{9,8},{10,11... | collective-permute-start | bytes 3145736 | tf_op jit(solution)/shard_map/ppermute | solution.py:33
  76.9 9.0 %collective-permute-start.30 = (bf16[128,1024]{1,0:T(8,128)(2,1)S(1)}, bf16[128,1024]{1,0:T(8,128)(2,1)S(1)}, u32[]{:S(2)}, u32[]{:S(2)}) collective-permute-start(bf16[128,1024]{1,0:T(8,128)(2,1)S(1)} %pad_maximum_fusion), channel_id=1, source_target_pairs={{0,64},{64,128},{128,192},{192,0},{1,65},{65,129},{129,193},{193,1... | collective-permute-start | bytes 786440 | tf_op jit(solution)/shard_map/ppermute | solution.py:47
  77.8 8.3 %collective-permute-start.32 = (bf16[128,1024]{1,0:T(8,128)(2,1)S(1)}, bf16[128,1024]{1,0:T(8,128)(2,1)S(1)}, u32[]{:S(2)}, u32[]{:S(2)}) collective-permute-start(bf16[128,1024]{1,0:T(8,128)(2,1)S(1)} %pad_maximum_fusion.1), channel_id=1, source_target_pairs={{0,192},{64,0},{128,64},{192,128},{1,193},{65,1},{129,65},{193,129... | collective-permute-start | bytes 786440 | tf_op jit(solution)/shard_map/ppermute | solution.py:47
  79.9 8.8 %collective-permute-start.21 = (bf16[4,2048]{1,0:T(4,128)(2,1)S(1)}, bf16[4,2048]{1,0:T(4,128)(2,1)S(1)}, u32[]{:S(2)}, u32[]{:S(2)}) collective-permute-start(bf16[4,2048]{1,0:T(4,128)(2,1)S(1)} %add_convert_fusion), channel_id=1, source_target_pairs={{0,8},{1,9},{2,10},{3,11},{4,12},{5,13},{6,14},{7,15},{8,0},{9,1},... | collective-permute-start | bytes 49160 | tf_op jit(solution)/shard_map/ppermute | solution.py:41
  86.3 4.4 %collective-permute-start.33 = (bf16[64,1024]{1,0:T(8,128)(2,1)S(1)}, bf16[64,1024]{1,0:T(8,128)(2,1)S(1)}, u32[]{:S(2)}, u32[]{:S(2)}) collective-permute-start(bf16[64,1024]{1,0:T(8,128)(2,1)S(1)} %slice.163), channel_id=1, source_target_pairs={{0,2},{1,15},{2,4},{3,1},{4,6},{5,3},{6,8},{7,5},{8,10},{9,7},{10,... | collective-permute-start | bytes 393224 | tf_op jit(solution)/shard_map/ppermute | solution.py:41
  88.8 5.3 %collective-permute-start.22 = (bf16[8,2048]{1,0:T(8,128)(2,1)S(1)}, bf16[8,2048]{1,0:T(8,128)(2,1)S(1)}, u32[]{:S(2)}, u32[]{:S(2)}) collective-permute-start(bf16[8,2048]{1,0:T(8,128)(2,1)S(1)} %pad_maximum_fusion.4), channel_id=1, source_target_pairs={{0,12},{1,5},{2,14},{3,7},{4,0},{5,9},{6,2},{7,11},{8,4},{9,13},{1... | collective-permute-start | bytes 98312 | tf_op jit(solution)/shard_map/ppermute | solution.py:41
  90.8 9.9 %collective-permute-start.34 = (bf16[32,1024]{1,0:T(8,128)(2,1)S(1)}, bf16[32,1024]{1,0:T(8,128)(2,1)S(1)}, u32[]{:S(2)}, u32[]{:S(2)}) collective-permute-start(bf16[32,1024]{1,0:T(8,128)(2,1)S(1)} %slice.164), channel_id=1, source_target_pairs={{0,4},{1,13},{2,6},{3,15},{4,8},{5,1},{6,10},{7,3},{8,12},{9,5},{1... | collective-permute-start | bytes 196616 | tf_op jit(solution)/shard_map/ppermute | solution.py:41
  94.1 8.8 %collective-permute-start.23 = (bf16[16,2048]{1,0:T(8,128)(2,1)S(1)}, bf16[16,2048]{1,0:T(8,128)(2,1)S(1)}, u32[]{:S(2)}, u32[]{:S(2)}) collective-permute-start(bf16[16,2048]{1,0:T(8,128)(2,1)S(1)} %pad_maximum_fusion.3), channel_id=1, source_target_pairs={{0,14},{1,3},{2,0},{3,5},{4,2},{5,7},{6,4},{7,9},{8,6},{9,11},{10,... | collective-permute-start | bytes 196616 | tf_op jit(solution)/shard_map/ppermute | solution.py:41
  96.2 46.2 %collective-permute-start.17 = (bf16[512,1024]{1,0:T(8,128)(2,1)S(1)}, bf16[512,1024]{1,0:T(8,128)(2,1)S(1)}, u32[]{:S(2)}, u32[]{:S(2)}) collective-permute-start(bf16[512,1024]{1,0:T(8,128)(2,1)S(1)} %shard_map.128), channel_id=1, source_target_pairs={{0,2},{1,63},{2,4},{3,1},{4,6},{5,3},{6,8},{7,5},{8,10},{9,7},{10,... | collective-permute-start | bytes 3145736 | tf_op jit(solution)/shard_map/ppermute | solution.py:52
  100.7 7.1 %collective-permute-start.35 = (bf16[16,1024]{1,0:T(8,128)(2,1)S(1)}, bf16[16,1024]{1,0:T(8,128)(2,1)S(1)}, u32[]{:S(2)}, u32[]{:S(2)}) collective-permute-start(bf16[16,1024]{1,0:T(8,128)(2,1)S(1)} %slice.166), channel_id=1, source_target_pairs={{0,8},{1,9},{2,10},{3,11},{4,12},{5,13},{6,14},{7,15},{8,0},{9,1},... | collective-permute-start | bytes 98312 | tf_op jit(solution)/shard_map/ppermute | solution.py:41
  102.9 4.9 %collective-permute-start.24 = (bf16[32,2048]{1,0:T(8,128)(2,1)S(1)}, bf16[32,2048]{1,0:T(8,128)(2,1)S(1)}, u32[]{:S(2)}, u32[]{:S(2)}) collective-permute-start(bf16[32,2048]{1,0:T(8,128)(2,1)S(1)} %pad_maximum_fusion.2.own_ref), channel_id=1, source_target_pairs={{0,48},{1,49},{2,50},{3,51},{4,52},{5,53},{6,54},{7,55},{8,56},{9,... | collective-permute-start | bytes 393224 | tf_op jit(solution)/shard_map/ppermute | solution.py:37
  104.3 16.7 %collective-permute-start.25 = (bf16[32,2048]{1,0:T(8,128)(2,1)S(1)}, bf16[32,2048]{1,0:T(8,128)(2,1)S(1)}, u32[]{:S(2)}, u32[]{:S(2)}) collective-permute-start(bf16[32,2048]{1,0:T(8,128)(2,1)S(1)} %pad_maximum_fusion.2.own_ref), channel_id=1, source_target_pairs={{0,32},{1,33},{2,34},{3,35},{4,36},{5,37},{6,38},{7,39},{8,40},{9,... | collective-permute-start | bytes 393224 | tf_op jit(solution)/shard_map/ppermute | solution.py:37
  107.8 13.3 %collective-permute-start.26 = (bf16[32,2048]{1,0:T(8,128)(2,1)S(1)}, bf16[32,2048]{1,0:T(8,128)(2,1)S(1)}, u32[]{:S(2)}, u32[]{:S(2)}) collective-permute-start(bf16[32,2048]{1,0:T(8,128)(2,1)S(1)} %pad_maximum_fusion.2.own_ref), channel_id=1, source_target_pairs={{0,16},{1,17},{2,18},{3,19},{4,20},{5,21},{6,22},{7,23},{8,24},{9,... | collective-permute-start | bytes 393224 | tf_op jit(solution)/shard_map/ppermute | solution.py:37
  107.9 13.5 %collective-permute-start.36 = (bf16[4,1024]{1,0:T(4,128)(2,1)S(1)}, bf16[4,1024]{1,0:T(4,128)(2,1)S(1)}, u32[]{:S(2)}, u32[]{:S(2)}) collective-permute-start(bf16[4,1024]{1,0:T(4,128)(2,1)S(1)} %get-tuple-element.52), channel_id=1, source_target_pairs={{0,16},{1,17},{2,18},{3,19},{4,20},{5,21},{6,22},{7,23},{8,24},{9,... | collective-permute-start | bytes 24584 | tf_op jit(solution)/shard_map/ppermute | solution.py:37
  120.9 21.4 %collective-permute-start.14 = (bf16[256,1024]{1,0:T(8,128)(2,1)S(1)}, bf16[256,1024]{1,0:T(8,128)(2,1)S(1)}, u32[]{:S(2)}, u32[]{:S(2)}) collective-permute-start(bf16[256,1024]{1,0:T(8,128)(2,1)S(1)} %get-tuple-element.32), channel_id=1, source_target_pairs={{0,62},{1,3},{2,0},{3,5},{4,2},{5,7},{6,4},{7,9},{8,6},{9,11},{10,... | collective-permute-start | bytes 1572872 | tf_op jit(solution)/shard_map/ppermute | solution.py:52
  121.1 21.2 %collective-permute-start.15 = (bf16[256,1024]{1,0:T(8,128)(2,1)S(1)}, bf16[256,1024]{1,0:T(8,128)(2,1)S(1)}, u32[]{:S(2)}, u32[]{:S(2)}) collective-permute-start(bf16[256,1024]{1,0:T(8,128)(2,1)S(1)} %get-tuple-element.33), channel_id=1, source_target_pairs={{0,62},{1,3},{2,0},{3,5},{4,2},{5,7},{6,4},{7,9},{8,6},{9,11},{10,... | collective-permute-start | bytes 1572872 | tf_op jit(solution)/shard_map/ppermute | solution.py:52
  121.4 3.0 %collective-permute-start.37 = (bf16[4,1024]{1,0:T(4,128)(2,1)S(1)}, bf16[4,1024]{1,0:T(4,128)(2,1)S(1)}, u32[]{:S(2)}, u32[]{:S(2)}) collective-permute-start(bf16[4,1024]{1,0:T(4,128)(2,1)S(1)} %get-tuple-element.54), channel_id=1, source_target_pairs={{0,48},{1,49},{2,50},{3,51},{4,52},{5,53},{6,54},{7,55},{8,56},{9,... | collective-permute-start | bytes 24584 | tf_op jit(solution)/shard_map/ppermute | solution.py:37
  124.4 4.9 %collective-permute-start.38 = (bf16[4,1024]{1,0:T(4,128)(2,1)S(1)}, bf16[4,1024]{1,0:T(4,128)(2,1)S(1)}, u32[]{:S(2)}, u32[]{:S(2)}) collective-permute-start(bf16[4,1024]{1,0:T(4,128)(2,1)S(1)} %get-tuple-element.53), channel_id=1, source_target_pairs={{0,32},{1,33},{2,34},{3,35},{4,36},{5,37},{6,38},{7,39},{8,40},{9,... | collective-permute-start | bytes 24584 | tf_op jit(solution)/shard_map/ppermute | solution.py:37
  129.3 14.8 %collective-permute-start.27 = (bf16[128,2048]{1,0:T(8,128)(2,1)S(1)}, bf16[128,2048]{1,0:T(8,128)(2,1)S(1)}, u32[]{:S(2)}, u32[]{:S(2)}) collective-permute-start(bf16[128,2048]{1,0:T(8,128)(2,1)S(1)} %shard_map.130.own_ref), channel_id=1, source_target_pairs={{0,1},{1,0},{2,3},{3,2},{4,5},{5,4},{6,7},{7,6},{8,9},{9,8},{10,11... | collective-permute-start | bytes 1572872 | tf_op jit(solution)/shard_map/ppermute | solution.py:33
